TPU v7x, 256 devices: a whole 4x4x8 slice. The times are simulated.
256 devices in a mesh: member: 16 (over x, y_hi, core), tensor: 16 (over z, y_lo).
Axes of the slice: x: 4, y: 4 (y_hi: 2, y_lo: 2; y = y_hi * 2 + y_lo), z: 8, core: 2. Of those that a mesh axis runs over, the one named last changes fastest.
Arguments:
- prompt_acts: bfloat16 [128, 5120], P(None, 'member'), may hold values from -6 to 6
- gate_weight: bfloat16 [5120, 13824], P('member', 'tensor'), may hold values from -0.078125 to 0.078125
- up_weight: bfloat16 [5120, 13824], P('member', 'tensor'), may hold values from -0.078125 to 0.078125
- down_weight: bfloat16 [13824, 5120], P('tensor', 'member'), may hold values from -0.0546875 to 0.0546875
- d_table: bfloat16 [256, 3, 4, 5120], P('member'), may hold values from -6 to 6
- f_table: bfloat16 [256, 3, 4, 13824], P('member', None, None, 'tensor'), may hold values from -6 to 6
- seeds: int32 [128], P('member'), may hold values from 0 to 15
- fitness: float32 [128], P('member'), may hold values from -6 to 6
Outputs:
- outputs: bfloat16 [128, 128, 5120], P('member', None, 'tensor')
- delta_gate: bfloat16 [5120, 13824], P('member', 'tensor')
- delta_up: bfloat16 [5120, 13824], P('member', 'tensor')
- delta_down: bfloat16 [13824, 5120], P('tensor', 'member')
Inputs may be any that keep to these rules, and one draw needn't show every extreme that they name: Member m uses row (m // 8) * 16 + seeds[m] of both tables, a row in its own group's block.
All inputs are finite; a program needn't handle non-finite values.
Results may differ from a plain program's by a relative error of at most 0.025.
Values may be sent and summed in bfloat16 or wider, within the bound.
A program may use at most 128 MiB of HBM per device.

v0:
```python
import math

import jax
import jax.numpy as jnp
from jax import lax
from jax.sharding import Mesh
from jax.sharding import PartitionSpec as P

D = 5120
FFW = 13824
MEMBER = ("member_0", "member_1", "member_2")
TENSOR = ("tensor_0", "tensor_1")


perturb_gain = 0.5


def sent_to_all(shard, axis):
    devices = lax.axis_size(axis)
    return lax.all_to_all(
        jnp.broadcast_to(shard[None], (devices, *shard.shape)), axis, 0, 0, tiled=True
    )


def joined_along(parts, dim):
    dims = list(parts.shape[1:])
    dims[dim] *= parts.shape[0]
    return jnp.moveaxis(parts, 0, dim).reshape(dims)


def gather_axes(shard, axes, dim):
    far, near = axes
    leading = sent_to_all(shard, far)
    parts = jnp.swapaxes(sent_to_all(leading, near), 0, 1)
    return joined_along(parts.reshape(-1, *shard.shape), dim)


def gather_directly(shard, axis, dim):
    return joined_along(sent_to_all(shard, axis), dim)


def filled_up(lines, devices):
    spare = -len(lines) % devices
    return jnp.pad(lines, [(0, spare)] + [(0, 0)] * (lines.ndim - 1))


def cut_along(shard, dim, devices):
    before, after = (shard.shape[:dim], shard.shape[dim + 1 :])
    return jnp.moveaxis(shard.reshape(*before, devices, -1, *after), dim, 0)


def sent_and_summed(shard, axis, dim):
    devices = lax.axis_size(axis)
    parts = lax.all_to_all(cut_along(shard, dim, devices), axis, 0, 0, tiled=True)
    return jnp.sum(parts.astype(jnp.float32), axis=0)


def sum_in_two_steps(shard, axes, dim):
    far, near = axes
    own = sent_and_summed(cut_along(shard, dim, lax.axis_size(far)), near, dim + 1)
    return jnp.sum(
        lax.all_to_all(own.astype(jnp.bfloat16), far, 0, 0, tiled=True).astype(jnp.float32), axis=0
    )


def sum_by_parts(shard, axes):
    lines = shard.reshape(-1, shard.shape[-1])
    padded = filled_up(lines, lax.axis_size(axes[0]) * lax.axis_size(axes[1]))
    whole = gather_axes(sum_in_two_steps(padded, axes, 0).astype(jnp.bfloat16), axes, 0)
    return lax.slice_in_dim(whole, 0, len(lines)).reshape(shard.shape).astype(jnp.float32)


def taken_together(shard, axis):
    return sent_to_all(shard, axis).sum(axis=0)


def scatter_axes(shard, axes, dim):
    if not axes:
        return shard
    nearer = lax.psum_scatter(shard, axes[0], scatter_dimension=dim, tiled=True)
    return scatter_axes(nearer, axes[1:], dim)


def shards(prompt_acts, gate_weight, up_weight, down_weight, d_table, f_table, seeds, fitness):
    members = seeds.shape[0]
    prompt_len = prompt_acts.shape[0]
    rank_size = d_table.shape[2]
    d_sel = jnp.take(d_table, seeds, axis=0)
    selected_factors = jnp.take(f_table, seeds, axis=0)
    d_slices = lax.all_to_all(d_sel, MEMBER, split_axis=3, concat_axis=0, tiled=True)
    f_all, fit_all = (
        gather_axes(selected_factors, (("member_0", "member_1"), "member_2"), 0),
        gather_axes(fitness.astype(jnp.bfloat16), (("member_0", "member_1"), "member_2"), 0).astype(
            fitness.dtype
        ),
    )
    population = fit_all.shape[0]
    gate_part = jnp.dot(prompt_acts, gate_weight, preferred_element_type=jnp.float32)
    up_part = jnp.dot(prompt_acts, up_weight, preferred_element_type=jnp.float32)
    prompt_full = gather_directly(prompt_acts, MEMBER, 1)
    gate_sum, up_sum = (
        sum_by_parts(gate_part.astype(jnp.bfloat16), (("member_0", "member_1"), "member_2")),
        sum_by_parts(up_part.astype(jnp.bfloat16), (("member_0", "member_1"), "member_2")),
    )
    in_factors = d_sel[:, :2].reshape(members * 2 * rank_size, D)
    proj_sum = jnp.dot(prompt_full, in_factors.T, preferred_element_type=jnp.float32)
    base_gate = gate_sum.astype(jnp.bfloat16)
    base_up = up_sum.astype(jnp.bfloat16)
    proj_inputs = (
        (proj_sum / math.sqrt(D)).astype(jnp.bfloat16).reshape(prompt_len, members, 2, rank_size)
    )
    perturbed = jnp.einsum(
        "pmkr,mkrf->mkpf", proj_inputs, selected_factors[:, :2], preferred_element_type=jnp.float32
    )
    gate = base_gate.astype(jnp.float32)[None] + perturb_gain * perturbed[:, 0]
    up = base_up.astype(jnp.float32)[None] + perturb_gain * perturbed[:, 1]
    hidden_state = (jax.nn.silu(gate) * up).astype(jnp.bfloat16)
    projection_here = jnp.einsum(
        "cdv,czv->cdz", hidden_state, selected_factors[:, 2], preferred_element_type=jnp.float32
    )
    proj_down = (taken_together(projection_here, TENSOR) / math.sqrt(FFW)).astype(jnp.bfloat16)
    hidden_rows = hidden_state.reshape(members * prompt_len, hidden_state.shape[2])
    partial_value = jnp.dot(
        hidden_rows,
        lax.all_gather(down_weight, MEMBER, axis=1, tiled=True),
        preferred_element_type=jnp.float32,
    )
    summed = scatter_axes(partial_value.astype(jnp.bfloat16), TENSOR, 1).astype(jnp.float32)
    local_column_range = summed.shape[1]
    col_start = lax.axis_index(TENSOR) * local_column_range
    out_factor = lax.dynamic_slice_in_dim(d_sel[:, 2], col_start, local_column_range, 2)
    down_noise_delta = perturb_gain * jnp.einsum(
        "mpr,mrd->mpd", proj_down, out_factor, preferred_element_type=jnp.float32
    )
    outputs = (summed.reshape(members, prompt_len, local_column_range) + down_noise_delta).astype(
        jnp.bfloat16
    )
    mean = jnp.sum(fit_all) / population
    spread = jnp.sum((fit_all - mean) ** 2) / population
    score = (fit_all - mean) / jnp.sqrt(spread + 1.0)
    weighted = (d_slices.astype(jnp.float32) * score[:, None, None, None]).astype(jnp.bfloat16)
    scale = 1.0 / math.sqrt(population * rank_size)
    width_cols = weighted.shape[3]
    hidden_cols = f_all.shape[3]
    w_gate = weighted[:, 0].reshape(population * rank_size, width_cols)
    w_up = weighted[:, 1].reshape(population * rank_size, width_cols)
    w_down = weighted[:, 2].reshape(population * rank_size, width_cols)
    f_gate = f_all[:, 0].reshape(population * rank_size, hidden_cols)
    f_up = f_all[:, 1].reshape(population * rank_size, hidden_cols)
    down_factor_columns = f_all[:, 2].reshape(population * rank_size, hidden_cols)
    delta_gate = (jnp.dot(w_gate.T, f_gate, preferred_element_type=jnp.float32) * scale).astype(
        jnp.bfloat16
    )
    delta_up = (jnp.dot(w_up.T, f_up, preferred_element_type=jnp.float32) * scale).astype(
        jnp.bfloat16
    )
    delta_down = (
        jnp.dot(down_factor_columns.T, w_down, preferred_element_type=jnp.float32) * scale
    ).astype(jnp.bfloat16)
    return (outputs, delta_gate, delta_up, delta_down)


def solution(mesh):
    split = Mesh(
        mesh.devices.reshape(4, 2, 2, 8, 2),
        ("member_0", "member_1", "member_2", "tensor_0", "tensor_1"),
    )
    placed = (
        P(None, MEMBER),
        P(MEMBER, TENSOR),
        P(MEMBER, TENSOR),
        P(TENSOR, MEMBER),
        P(MEMBER, None, None, None),
        P(MEMBER, None, None, TENSOR),
        P(MEMBER),
        P(MEMBER),
    )
    return jax.shard_map(
        shards,
        mesh=split,
        in_specs=placed,
        out_specs=(
            P(MEMBER, None, TENSOR),
            P(MEMBER, TENSOR),
            P(MEMBER, TENSOR),
            P(TENSOR, MEMBER),
        ),
        check_vma=False,
    )
```

profile of v0, /device:TPU:1, one launch (start us, length us, event | category | flops | bytes accessed | tf_op | source)
XLA Modules:
  0.0 367.6 jit_solution(5300602378496376444)
XLA Ops:
  7.2 0.7 all-gather.2.cloned.1.call-update
  7.9 1.5 convolution_convert_fusion.1
  9.6 0.7 copy.151
  10.3 6.6 %all-to-all-start.5 = ((bf16[2,8,8,864]{3,2,1,0:T(8,128)(2,1)}), bf16[2,8,8,864]{3,2,1,0:T(8,128)(2,1)S(1)}, u32[]{:S(2)}, u32[]{:S(2)}) async-start(bf16[2,8,8,864]{3,2,1,0:T(8,128)(2,1)} %copy.151), calls=%async_computation.5 | async-start | bytes 458752 | tf_op jit(solution)/shard_map/all_to_all | solution.py:54
  17.0 1.5 convolution_convert_fusion.2
  18.7 0.7 copy.144
  19.4 3.5 all-to-all-start
  22.8 0.7 reduce_sum.77
  24.0 4.9 %all-to-all-start.6 = ((bf16[8,8,864]{2,1,0:T(8,128)(2,1)}), bf16[8,8,864]{2,1,0:T(8,128)(2,1)S(1)}, u32[]{:S(2)}, u32[]{:S(2)}) async-start(bf16[8,8,864]{2,1,0:T(8,128)(2,1)} %reduce_sum.77), calls=%async_computation.6 | async-start | bytes 229376 | tf_op jit(solution)/shard_map/all_to_all | solution.py:62
  28.9 0.7 reduce_sum.75
  29.6 6.7 %all-to-all-done.6 = bf16[8,8,864]{2,1,0:T(8,128)(2,1)S(1)} async-done(((bf16[8,8,864]{2,1,0:T(8,128)(2,1)}), bf16[8,8,864]{2,1,0:T(8,128)(2,1)S(1)}, u32[]{:S(2)}, u32[]{:S(2)}) %all-to-all-start.6) | async-done | bytes 110624 | tf_op jit(solution)/shard_map/all_to_all | solution.py:62
  36.3 3.7 %all-to-all-start.1 = ((bf16[8,8,864]{2,1,0:T(8,128)(2,1)}), bf16[8,8,864]{2,1,0:T(8,128)(2,1)S(1)}, u32[]{:S(2)}, u32[]{:S(2)}) async-start(bf16[8,8,864]{2,1,0:T(8,128)(2,1)} %reduce_sum.75), calls=%async_computation.1 | async-start | bytes 229376 | tf_op jit(solution)/shard_map/all_to_all | solution.py:62
  40.1 6.7 %all-to-all-done.1 = bf16[8,8,864]{2,1,0:T(8,128)(2,1)S(1)} async-done(((bf16[8,8,864]{2,1,0:T(8,128)(2,1)}), bf16[8,8,864]{2,1,0:T(8,128)(2,1)S(1)}, u32[]{:S(2)}, u32[]{:S(2)}) %all-to-all-start.1) | async-done | bytes 110624 | tf_op jit(solution)/shard_map/all_to_all | solution.py:62
  46.8 0.7 broadcast_in_dim.52
  47.5 3.4 all-to-all-start.7
  50.9 6.6 %all-to-all-done.7 = bf16[8,8,864]{2,1,0:T(8,128)(2,1)S(1)} async-done(((bf16[8,8,864]{2,1,0:T(8,128)(2,1)}), bf16[8,8,864]{2,1,0:T(8,128)(2,1)S(1)}, u32[]{:S(2)}, u32[]{:S(2)}) %all-to-all-start.7) | async-done | bytes 110624 | tf_op jit(solution)/shard_map/all_to_all | solution.py:20
  57.5 7.6 %all_to_all.80 = bf16[2,8,8,864]{3,2,1,0:T(8,128)(2,1)S(1)} all-to-all(bf16[2,8,8,864]{3,2,1,0:T(8,128)(2,1)S(1)} %broadcast_in_dim.53), channel_id=1, replica_groups=mesh['member_0'=4,'member_1'=2,'member_2'=2,'tensor_0'=8,'tensor_1'=2] {..., dimensions={0} | all-to-all | bytes 442368 | tf_op jit(solution)/shard_map/all_to_all | solution.py:20
  65.1 0.7 broadcast_in_dim.44
  65.8 3.4 all-to-all-start.2
  69.2 2.3 gather_fusion
  71.5 4.6 %all-to-all-done.2 = bf16[8,8,864]{2,1,0:T(8,128)(2,1)S(1)} async-done(((bf16[8,8,864]{2,1,0:T(8,128)(2,1)}), bf16[8,8,864]{2,1,0:T(8,128)(2,1)S(1)}, u32[]{:S(2)}, u32[]{:S(2)}) %all-to-all-start.2) | async-done | bytes 110624 | tf_op jit(solution)/shard_map/all_to_all | solution.py:20
  76.1 6.1 %all_to_all.81 = bf16[2,8,8,864]{3,2,1,0:T(8,128)(2,1)} all-to-all(bf16[2,8,8,864]{3,2,1,0:T(8,128)(2,1)S(1)} %broadcast_in_dim.45), channel_id=1, replica_groups=mesh['member_0'=4,'member_1'=2,'member_2'=2,'tensor_0'=8,'tensor_1'=2] {..., dimensions={0} | all-to-all | bytes 442368 | tf_op jit(solution)/shard_map/all_to_all | solution.py:20
  82.2 1.3 broadcast_in_dim.49
  83.5 3.9 %all-to-all-start.4 = ((bf16[16,128,320]{1,2,0:T(8,128)(2,1)}), bf16[16,128,320]{1,2,0:T(8,128)(2,1)S(1)}, u32[]{:S(2)}, u32[]{:S(2)}) async-start(bf16[16,128,320]{1,2,0:T(8,128)(2,1)} %broadcast_in_dim.49), calls=%async_computation.4 | async-start | bytes 2621440 | tf_op jit(solution)/shard_map/all_to_all | solution.py:20
  87.6 1.7 broadcast_select_fusion
  89.3 0.7 gather_fusion.1
  90.0 1.1 slice.52
  91.1 1.5 reshape.108
  92.6 0.8 broadcast_select_fusion.1
  93.5 1.0 copy.181
  94.5 1.0 convert_bitcast_fusion.2
  95.5 1.0 copy.180
  96.4 14.3 %all-to-all-done.4 = bf16[16,128,320]{1,2,0:T(8,128)(2,1)S(1)} async-done(((bf16[16,128,320]{1,2,0:T(8,128)(2,1)}), bf16[16,128,320]{1,2,0:T(8,128)(2,1)S(1)}, u32[]{:S(2)}, u32[]{:S(2)}) %all-to-all-start.4) | async-done | bytes 1310752 | tf_op jit(solution)/shard_map/all_to_all | solution.py:20
  111.1 2.1 fusion.18
  113.5 3.8 %copy.156 = f32[8,1,128,864]{2,0,3,1:T(8,128)} copy(f32[8,1,128,864]{2,3,1,0:T(8,128)S(1)} %slice_multiply_fusion) | data formatting | bytes 7077888 | tf_op jit(solution)/shard_map/mul | solution.py:116
  117.6 3.8 %copy.149 = f32[8,1,128,864]{2,0,3,1:T(8,128)} copy(f32[8,1,128,864]{2,3,0,1:T(8,128)S(1)} %fusion.2) | data formatting | bytes 7077888 | tf_op jit(solution)/shard_map/mul | solution.py:115
  121.4 2.1 add.60.clone
  123.5 2.0 add.55.clone
  125.5 25.7 %convolution_convert_fusion = bf16[1024,5120]{1,0:T(8,128)(2,1)} fusion(bf16[864,5120]{0,1:T(8,128)(2,1)} %all-gather.2.cloned.1.call-done, f32[108,8,8,128]{3,2,1,0:T(8,128)} %bitcast.163, f32[108,8,8,128]{3,2,1,0:T(8,128)} %bitcast.165, f32[108,8,8,128]{3,2,1,0:T(8,128)} %bitcast.164, f32[108,8,8,128]{3,2,1,0:T(8,128)} %bitcast.166), kind=kOutput, calls=%fused_computation.2 | convolution fusion | flops 9072017408 | bytes 33488896 | tf_op jit(solution)/shard_map/dot_general | solution.py:123
  151.2 14.4 %copy.171 = bf16[1024,5120]{0,1:T(8,128)(2,1)} copy(bf16[1024,5120]{1,0:T(8,128)(2,1)} %convolution_convert_fusion) | data formatting | bytes 20971520
  165.6 0.6 copy-done.13
  166.8 6.2 %all-to-all-start.11 = ((bf16[8,1,8]{2,1,0:T(2,128)(2,1)}), bf16[8,1,8]{2,1,0:T(2,128)(2,1)S(1)}, u32[]{:S(2)}, u32[]{:S(2)}) async-start(bf16[8,1,8]{2,1,0:T(2,128)(2,1)} %broadcast_in_dim.98), calls=%async_computation.11 | async-start | bytes 8192 | tf_op jit(solution)/shard_map/all_to_all | solution.py:20
  173.1 15.0 %copy.161 = bf16[8,3,4,5120]{0,2,1,3:T(4,128)(2,1)} copy(bf16[8,3,4,5120]{3,2,1,0:T(4,128)(2,1)S(1)} %broadcast_select_fusion) | data formatting | bytes 1966080 | tf_op jit(solution)/shard_map/jit(_take)/select_n | solution.py:88
  188.1 20.0 %reshape.151 = bf16[16,2,15360]{2,1,0:T(2,128)(2,1)} reshape(bf16[5120,3,4,8]{3,2,1,0:T(4,128)(2,1)} %bitcast.156) | data formatting | bytes 1966080
  208.1 4.2 %all_to_all.82 = bf16[2,8,8]{2,1,0:T(8,128)(2,1)S(1)} all-to-all(bf16[2,8,8]{2,1,0:T(8,128)(2,1)S(1)} %broadcast_in_dim.100), channel_id=1, replica_groups=mesh['member_0'=4,'member_1'=2,'member_2'=2,'tensor_0'=8,'tensor_1'=2] {..., dimensions={0} | all-to-all | bytes 512 | tf_op jit(solution)/shard_map/all_to_all | solution.py:20
  212.3 7.5 %all-to-all-start.10 = ((bf16[16,2,15360]{2,1,0:T(2,128)(2,1)}), bf16[16,2,15360]{2,1,0:T(2,128)(2,1)S(1)}, u32[]{:S(2)}, u32[]{:S(2)}) async-start(bf16[16,2,15360]{2,1,0:T(2,128)(2,1)} %reshape.151), calls=%async_computation.10 | async-start | bytes 1966080 | tf_op jit(solution)/shard_map/all_to_all | solution.py:90
  219.9 16.1 %all-to-all-done.10 = bf16[16,2,15360]{2,1,0:T(2,128)(2,1)S(1)} async-done(((bf16[16,2,15360]{2,1,0:T(2,128)(2,1)}), bf16[16,2,15360]{2,1,0:T(2,128)(2,1)S(1)}, u32[]{:S(2)}, u32[]{:S(2)}) %all-to-all-start.10) | async-done | bytes 983072 | tf_op jit(solution)/shard_map/all_to_all | solution.py:90
  236.0 1.2 broadcast_in_dim.101
  237.2 4.3 %all-to-all-start.13 = ((bf16[8,8,3,4,864]{4,1,3,2,0:T(8,128)(2,1)}), bf16[8,8,3,4,864]{4,1,3,2,0:T(8,128)(2,1)}, u32[]{:S(2)}, u32[]{:S(2)}) async-start(bf16[8,8,3,4,864]{4,1,3,2,0:T(8,128)(2,1)} %broadcast_in_dim.101), calls=%async_computation.13 | async-start | bytes 2752512 | tf_op jit(solution)/shard_map/all_to_all | solution.py:20
  241.6 40.0 %reduce-scatter.7.cloned.1.call-done = bf16[640,1024]{1,0:T(8,128)(2,1)} async-done(((bf16[5120,1024]{1,0:T(8,128)(2,1)}), bf16[640,1024]{1,0:T(8,128)(2,1)}) %reduce-scatter.7.cloned.1.call-update) | async-done | bytes 1310736
  284.3 19.3 %reshape.152 = bf16[5120,3,4,8]{3,2,1,0:T(4,128)(2,1)} reshape(bf16[16,2,15360]{2,1,0:T(2,128)(2,1)S(1)} %all-to-all-done.10) | data formatting | bytes 1966080
  303.6 21.0 %copy.162 = f32[8,3,4,16,320]{4,0,3,2,1:T(8,128)} copy(bf16[8,3,4,16,320]{0,2,1,4,3:T(4,128)(2,1)} %bitcast.155) | data formatting | bytes 2949120 | tf_op jit(solution)/shard_map/convert_element_type | solution.py:141
  324.6 2.0 copy.164
  326.9 1.9 copy.166
  329.2 6.7 %all_to_all.83 = bf16[2,8,8,3,4,864]{5,2,1,4,3,0:T(8,128)(2,1)S(1)} all-to-all(bf16[2,8,8,3,4,864]{5,2,1,4,3,0:T(8,128)(2,1)S(1)} %broadcast_in_dim.102), channel_id=1, replica_groups=mesh['member_0'=4,'member_1'=2,'member_2'=2,'tensor_0'=8,'tensor_1'=2] {..., dimensions={0} | all-to-all | bytes 5308416 | tf_op jit(solution)/shard_map/all_to_all | solution.py:20
  336.2 1.3 fusion.16
  337.5 1.4 slice-done.1
  339.0 2.3 fusion.7
  341.3 0.7 broadcast_in_dim.54
  342.0 5.2 %all-to-all-start.9 = ((f32[16,8,128,4]{2,1,3,0:T(8,128)}), f32[16,8,128,4]{2,1,3,0:T(8,128)S(1)}, u32[]{:S(2)}, u32[]{:S(2)}) async-start(f32[16,8,128,4]{2,1,3,0:T(8,128)} %broadcast_in_dim.54), calls=%async_computation.9 | async-start | bytes 524288 | tf_op jit(solution)/shard_map/all_to_all | solution.py:20
  347.3 2.6 fusion.15
  349.9 2.6 fusion.14
  352.5 6.0 %all-to-all-done.9 = f32[16,8,128,4]{2,1,3,0:T(8,128)S(1)} async-done(((f32[16,8,128,4]{2,1,3,0:T(8,128)}), f32[16,8,128,4]{2,1,3,0:T(8,128)S(1)}, u32[]{:S(2)}, u32[]{:S(2)}) %all-to-all-start.9) | async-done | bytes 262176 | tf_op jit(solution)/shard_map/all_to_all | solution.py:20
  358.5 2.5 fusion.13
  (75 shorter events, 5.2 us)
Async XLA Ops:
  7.2 62.0 %copy-start = (bf16[16,3,4,5120]{3,2,1,0:T(4,128)(2,1)S(1)}, bf16[16,3,4,5120]{3,2,1,0:T(4,128)(2,1)}, u32[]{:S(2)}) copy-start(bf16[16,3,4,5120]{3,2,1,0:T(4,128)(2,1)} %param.12) | copy-start | bytes 5898244
  7.2 32.9 %copy-start.12 = (s32[8]{0:T(128)S(1)}, s32[8]{0:T(128)}, u32[]{:S(2)}) copy-start(s32[8]{0:T(128)} %param.14) | copy-start | bytes 100
  7.2 114.2 %all-gather.2.cloned.1.call-start = ((), (), s32[]{:S(2)}) async-start(), calls=%async_computation.17 | async-start | bytes 9748480 | tf_op jit(solution)/shard_map/all_gather | solution.py:125
  10.3 9.0 %all-to-all-start.5 = ((bf16[2,8,8,864]{3,2,1,0:T(8,128)(2,1)}), bf16[2,8,8,864]{3,2,1,0:T(8,128)(2,1)S(1)}, u32[]{:S(2)}, u32[]{:S(2)}) async-start(bf16[2,8,8,864]{3,2,1,0:T(8,128)(2,1)} %copy.151), calls=%async_computation.5 | async-start | bytes 458752 | tf_op jit(solution)/shard_map/all_to_all | solution.py:54
  18.5 63.7 %copy-start.10 = (bf16[128,320]{0,1:T(8,128)(2,1)S(1)}, bf16[128,320]{0,1:T(8,128)(2,1)}, u32[]{:S(2)}) copy-start(bf16[128,320]{0,1:T(8,128)(2,1)} %param.8) | copy-start | bytes 245764
  19.4 4.6 %all-to-all-start = ((bf16[2,8,8,864]{3,2,1,0:T(8,128)(2,1)}), bf16[2,8,8,864]{3,2,1,0:T(8,128)(2,1)S(1)}, u32[]{:S(2)}, u32[]{:S(2)}) async-start(bf16[2,8,8,864]{3,2,1,0:T(8,128)(2,1)} %copy.144), calls=%async_computation | async-start | bytes 458752 | tf_op jit(solution)/shard_map/all_to_all | solution.py:54
  24.0 12.3 %all-to-all-start.6 = ((bf16[8,8,864]{2,1,0:T(8,128)(2,1)}), bf16[8,8,864]{2,1,0:T(8,128)(2,1)S(1)}, u32[]{:S(2)}, u32[]{:S(2)}) async-start(bf16[8,8,864]{2,1,0:T(8,128)(2,1)} %reduce_sum.77), calls=%async_computation.6 | async-start | bytes 229376 | tf_op jit(solution)/shard_map/all_to_all | solution.py:62
  36.3 10.5 %all-to-all-start.1 = ((bf16[8,8,864]{2,1,0:T(8,128)(2,1)}), bf16[8,8,864]{2,1,0:T(8,128)(2,1)S(1)}, u32[]{:S(2)}, u32[]{:S(2)}) async-start(bf16[8,8,864]{2,1,0:T(8,128)(2,1)} %reduce_sum.75), calls=%async_computation.1 | async-start | bytes 229376 | tf_op jit(solution)/shard_map/all_to_all | solution.py:62
  47.5 10.0 %all-to-all-start.7 = ((bf16[8,8,864]{2,1,0:T(8,128)(2,1)}), bf16[8,8,864]{2,1,0:T(8,128)(2,1)S(1)}, u32[]{:S(2)}, u32[]{:S(2)}) async-start(bf16[8,8,864]{2,1,0:T(8,128)(2,1)} %broadcast_in_dim.52), calls=%async_computation.7 | async-start | bytes 229376 | tf_op jit(solution)/shard_map/all_to_all | solution.py:20
  65.8 10.3 %all-to-all-start.2 = ((bf16[8,8,864]{2,1,0:T(8,128)(2,1)}), bf16[8,8,864]{2,1,0:T(8,128)(2,1)S(1)}, u32[]{:S(2)}, u32[]{:S(2)}) async-start(bf16[8,8,864]{2,1,0:T(8,128)(2,1)} %broadcast_in_dim.44), calls=%async_computation.2 | async-start | bytes 229376 | tf_op jit(solution)/shard_map/all_to_all | solution.py:20
  71.5 17.8 %copy-start.11 = (bf16[16,3,4,864]{3,2,1,0:T(4,128)(2,1)S(1)}, bf16[16,3,4,864]{3,2,1,0:T(4,128)(2,1)}, u32[]{:S(2)}) copy-start(bf16[16,3,4,864]{3,2,1,0:T(4,128)(2,1)} %param.13) | copy-start | bytes 995332
  83.5 27.2 %all-to-all-start.4 = ((bf16[16,128,320]{1,2,0:T(8,128)(2,1)}), bf16[16,128,320]{1,2,0:T(8,128)(2,1)S(1)}, u32[]{:S(2)}, u32[]{:S(2)}) async-start(bf16[16,128,320]{1,2,0:T(8,128)(2,1)} %broadcast_in_dim.49), calls=%async_computation.4 | async-start | bytes 2621440 | tf_op jit(solution)/shard_map/all_to_all | solution.py:20
  87.4 194.2 %reduce-scatter.7.cloned.1.call-start = ((), (), s32[]{:S(2)}) async-start(), calls=%async_computation.18 | async-start | bytes 11796480
  89.3 192.3 %copy-start.3 = (bf16[8,3,4,5120]{3,2,1,0:T(4,128)(2,1)}, bf16[8,3,4,5120]{3,2,1,0:T(4,128)(2,1)S(1)}, u32[]{:S(2)}) copy-start(bf16[8,3,4,5120]{3,2,1,0:T(4,128)(2,1)S(1)} %broadcast_select_fusion) | copy-start | bytes 2949124
  113.2 4.1 %copy-start.2 = (f32[8,2,128,864]{2,3,1,0:T(8,128)}, f32[8,2,128,864]{2,3,1,0:T(8,128)S(1)}, u32[]{:S(2)}) copy-start(f32[8,2,128,864]{2,3,1,0:T(8,128)S(1)} %fusion.18) | copy-start | bytes 21233668
  117.6 3.8 %copy-start.5 = (f32[128,864]{0,1:T(8,128)S(1)}, f32[128,864]{0,1:T(8,128)}, u32[]{:S(2)}) copy-start(f32[128,864]{0,1:T(8,128)} %copy.181) | copy-start | bytes 1327108
  121.4 2.1 copy-start.6
  165.6 0.7 copy-start.13
  166.8 41.3 %all-to-all-start.11 = ((bf16[8,1,8]{2,1,0:T(2,128)(2,1)}), bf16[8,1,8]{2,1,0:T(2,128)(2,1)S(1)}, u32[]{:S(2)}, u32[]{:S(2)}) async-start(bf16[8,1,8]{2,1,0:T(2,128)(2,1)} %broadcast_in_dim.98), calls=%async_computation.11 | async-start | bytes 8192 | tf_op jit(solution)/shard_map/all_to_all | solution.py:20
  188.1 31.7 %copy-start.8 = (bf16[8,3,4,864]{3,2,1,0:T(4,128)(2,1)S(1)}, bf16[8,3,4,864]{3,2,1,0:T(4,128)(2,1)}, u32[]{:S(2)}) copy-start(bf16[8,3,4,864]{3,2,1,0:T(4,128)(2,1)} %broadcast_select_fusion.1) | copy-start | bytes 497668
  212.3 23.7 %all-to-all-start.10 = ((bf16[16,2,15360]{2,1,0:T(2,128)(2,1)}), bf16[16,2,15360]{2,1,0:T(2,128)(2,1)S(1)}, u32[]{:S(2)}, u32[]{:S(2)}) async-start(bf16[16,2,15360]{2,1,0:T(2,128)(2,1)} %reshape.151), calls=%async_computation.10 | async-start | bytes 1966080 | tf_op jit(solution)/shard_map/all_to_all | solution.py:90
  237.2 89.6 %all-to-all-start.13 = ((bf16[8,8,3,4,864]{4,1,3,2,0:T(8,128)(2,1)}), bf16[8,8,3,4,864]{4,1,3,2,0:T(8,128)(2,1)}, u32[]{:S(2)}, u32[]{:S(2)}) async-start(bf16[8,8,3,4,864]{4,1,3,2,0:T(8,128)(2,1)} %broadcast_in_dim.101), calls=%async_computation.13 | async-start | bytes 2752512 | tf_op jit(solution)/shard_map/all_to_all | solution.py:20
  241.5 117.0 %reduce-scatter.9.cloned.1.call-start = ((), (), s32[]{:S(2)}) async-start(), calls=%async_computation.19 | async-start | bytes 1966080
  326.9 9.3 %copy-start.9 = (bf16[128,3,4,320]{0,3,2,1:T(8,128)(2,1)}, bf16[128,3,4,320]{0,3,2,1:T(8,128)(2,1)S(1)}, u32[]{:S(2)}) copy-start(bf16[128,3,4,320]{0,3,2,1:T(8,128)(2,1)S(1)} %multiply_convert_fusion) | copy-start | bytes 2949124
  329.2 8.3 %slice-start = ((s8[7077888]{0:T(1024)(128)(4,1)}), s8[4194304]{0:T(1024)(128)(4,1)S(1)}, s32[]{:S(2)}) async-start(s8[7077888]{0:T(1024)(128)(4,1)} %bitcast.158), calls=%async_computation.20 | async-start | bytes 8388608
  335.9 3.0 slice-start.1
  335.9 3.1 copy-start.7
  336.1 5.1 %copy-start.4 = (bf16[8,2,8,3,4,864]{5,2,1,0,4,3:T(8,128)(2,1)}, bf16[8,2,8,3,4,864]{5,2,1,0,4,3:T(8,128)(2,1)S(1)}, u32[]{:S(2)}) copy-start(bf16[8,2,8,3,4,864]{5,2,1,0,4,3:T(8,128)(2,1)S(1)} %copy.167) | copy-start | bytes 7962628
  341.3 17.2 %slice-start.2 = ((bf16[8,3,4,5120]{3,2,1,0:T(4,128)(2,1)}), bf16[8,1,4,5120]{3,2,1,0:T(4,128)(2,1)S(1)}, s32[]{:S(2)}) async-start(bf16[8,3,4,5120]{3,2,1,0:T(4,128)(2,1)} %copy-done.3), calls=%async_computation.22 | async-start | bytes 655360 | tf_op jit(solution)/shard_map/slice | solution.py:131
  341.3 19.7 %copy-start.1 = (bf16[16,3,4,5120]{3,2,1,0:T(4,128)(2,1)S(1)}, bf16[16,3,4,5120]{3,2,1,0:T(4,128)(2,1)}, u32[]{:S(2)}) copy-start(bf16[16,3,4,5120]{3,2,1,0:T(4,128)(2,1)} %param.12) | copy-start | bytes 5898244
  342.0 16.4 %all-to-all-start.9 = ((f32[16,8,128,4]{2,1,3,0:T(8,128)}), f32[16,8,128,4]{2,1,3,0:T(8,128)S(1)}, u32[]{:S(2)}, u32[]{:S(2)}) async-start(f32[16,8,128,4]{2,1,3,0:T(8,128)} %broadcast_in_dim.54), calls=%async_computation.9 | async-start | bytes 524288 | tf_op jit(solution)/shard_map/all_to_all | solution.py:20
Sparse Core Ops, SparseCore 0:
  10.7 96.9 all-gather.1
  165.7 115.8 reduce-scatter.6
  284.1 26.8 reduce-scatter.8
where the time goes:
time: 371 us; the launch traced here: 368 us
  local copies, waits for them, and re-layouts  123 us (33%)
  waiting for transfers between devices  102 us (27%)
  starting transfers between devices  52.9 us (14%)
  matrix products  42.5 us (11%)
  blocking collectives  24.6 us (7%)
  between operations  15.5 us (4%)
  other arithmetic  6.97 us (2%)
    unnamed x38, local copies, waits for them, and re-layouts  57.7 us
    unnamed x5, waiting for transfers between devices  40.8 us
    all_to_all x6, waiting for transfers between devices, sent_to_all(): lax.all_to_all(jnp.broadcast_to(shard[None], (devices, *shard.shape)), ax...  31.5 us
    all_to_all x6, starting transfers between devices, sent_to_all(): lax.all_to_all(jnp.broadcast_to(shard[None], (devices, *shard.shape)), ax...  26.3 us
    dot_general x1, matrix products, shards(): jnp.dot(hidden_rows, lax.all_gather(down_weight, MEMBER, axis=1, tiled=Tr...  25.7 us
    all_to_all x4, blocking collectives, sent_to_all(): lax.all_to_all(jnp.broadcast_to(shard[None], (devices, *shard.shape)), ax...  24.6 us
    convert_element_type x2, local copies, waits for them, and re-layouts, shards(): d_slices.astype(jnp.float32) * score[:, None, None, None]  23.1 us
    all_to_all x1, waiting for transfers between devices, shards(): lax.all_to_all(d_sel, MEMBER, split_axis=3, concat_axis=0, tiled=True)  16.1 us
  transfers between devices with their start and end apart: 14, of which 9 were waited for; matrix products, arithmetic and copies ran while one was open for 34% of the time, Pallas kernels for 0%

commit v1 on v0

v1 whole, which is shorter than its diff:
```python
import functools
import math

import jax
import jax.numpy as jnp
from jax import lax
from jax.experimental import pallas as pl
from jax.experimental.pallas import tpu as pltpu
from jax.sharding import Mesh
from jax.sharding import PartitionSpec as P

D = 5120
FFW = 13824
FB = 864
FP = 896
AX = ("x", "yh", "c", "z", "yl")
MEMBER = ("x", "yh", "c")
TENSOR = ("z", "yl")
MESH = pl.DeviceIdType.MESH
BF = jnp.bfloat16
F32 = jnp.float32


def rcopy(src, dst, ss, rs, dev):
    return pltpu.make_async_remote_copy(
        src_ref=src, dst_ref=dst, send_sem=ss, recv_sem=rs, device_id=dev, device_id_type=MESH
    )


def at(x, yh, c, z, yl):
    return {"x": x, "yh": yh, "c": c, "z": z, "yl": yl}


def k1(
    dt_ref, base_ref, f_ref, pt_ref, a2_ref, out_ref,
    dbuf, hbuf, pd, snd, rcv, fin, fsnd, ft,
    ys, yr, yloc, xs_s, xs_r, ds_s, ds_r, rs_s, rs_r, fs_s, fs_r,
):
    x, yh, c, z, yl = [lax.axis_index(a) for a in AX]
    sgn = 1 - 2 * c
    xn, xp = lax.rem(x + sgn + 4, 4), lax.rem(x - sgn + 4, 4)
    zn, zp = lax.rem(z + sgn + 8, 8), lax.rem(z - sgn + 8, 8)
    ypeers = [at(x, h, yl, z, c) for h in range(2)]
    me_y = [(h == yh) & (c == yl) for h in range(2)]
    partner = at(x, yh, 1 - c, z, yl)
    ypart = at(x, 1 - yh, c, z, yl)

    barrier = pltpu.get_barrier_semaphore()
    others = [partner, ypart, at(xn, yh, c, z, yl), at(xp, yh, c, z, yl), at(x, yh, c, zn, yl), at(x, yh, c, zp, yl)]
    for o in others:
        pl.semaphore_signal(barrier, inc=1, device_id=o, device_id_type=MESH)
    for h in range(2):
        @pl.when(jnp.logical_not(me_y[h]))
        def _():
            pl.semaphore_signal(barrier, inc=1, device_id=ypeers[h], device_id_type=MESH)
    @pl.when(c == yl)
    def _():
        pl.semaphore_wait(barrier, 7)
    @pl.when(c != yl)
    def _():
        pl.semaphore_wait(barrier, 8)

    for h in range(2):
        @pl.when(jnp.logical_not(me_y[h]))
        def _():
            rcopy(dt_ref.at[h], dbuf.at[yl, 2 * x + yh], ys.at[h], yr.at[yh], ypeers[h]).start()
        @pl.when(me_y[h])
        def _():
            pltpu.make_async_copy(dt_ref.at[h], dbuf.at[yl, 2 * x + yh], yloc).start()

    def wait_y():
        for h in range(2):
            @pl.when(jnp.logical_not(me_y[h]))
            def _():
                rcopy(dt_ref.at[h], dbuf.at[c, 2 * x + h], ys.at[h], yr.at[h], ypeers[h]).wait_recv()
            @pl.when(me_y[h])
            def _():
                pltpu.make_async_copy(dt_ref.at[h], dbuf.at[yl, 2 * x + yh], yloc).wait()

    def blk(core, xi):
        return dbuf.at[core, pl.ds(2 * xi, 2)]

    def xfwd(s):
        xi = lax.rem(x - sgn * s + 8, 4)
        rcopy(blk(c, xi), blk(c, xi), xs_s.at[s], xs_r.at[s], at(xn, yh, c, z, yl)).start()

    def dfwd(s):
        xi = lax.rem(x - sgn * s + 8, 4)
        rcopy(blk(c, xi), blk(c, xi), ds_s.at[s], ds_r.at[s], partner).start()

    def wait_x(s):
        xi = lax.rem(x - sgn * (s + 1) + 8, 4)
        rcopy(blk(c, xi), blk(c, xi), xs_s.at[s], xs_r.at[s], at(xn, yh, c, z, yl)).wait_recv()

    def wait_d(s):
        xi = lax.rem(x + sgn * s + 8, 4)
        rcopy(blk(1 - c, xi), blk(1 - c, xi), ds_s.at[s], ds_r.at[s], partner).wait_recv()

    for g in range(2):
        for t in range(2):
            for k in range(2):
                ft[g, t, k] = f_ref[g, t, k].T

    wait_y()
    xfwd(0)
    dfwd(0)

    rowm = lax.broadcasted_iota(jnp.int32, (32, 256), 0) // 4
    lanem = lax.broadcasted_iota(jnp.int32, (32, 256), 1) // 128

    def hidden(i):
        g, cc = i // 4, lax.rem(i, 4)
        live = rowm == 2 * cc + lanem
        pm = [
            jnp.where(live, jnp.concatenate([pt_ref[g, k]] * 2, axis=1).astype(F32), 0.0).astype(BF)
            for k in range(2)
        ]
        for t in range(2):
            def rows(rb, _):
                r = pl.ds(pl.multiple_of(rb * 64, 64), 64)
                b = [base_ref[t, k, r].astype(F32) for k in range(2)]
                gu = [
                    jnp.concatenate([b[k], b[k]], axis=1)
                    + jnp.dot(ft[g, t, k, r], pm[k], preferred_element_type=F32)
                    for k in range(2)
                ]
                hbuf[i, t, r] = (gu[0] / (1.0 + jnp.exp(-gu[0])) * gu[1]).astype(BF)
                return 0
            lax.fori_loop(0, 14, rows, 0)
        q = jnp.dot(f_ref[g, 0, 2], hbuf[i, 0], preferred_element_type=F32)
        q += jnp.dot(f_ref[g, 1, 2], hbuf[i, 1], preferred_element_type=F32)
        pd[i] = jnp.where(live, q * (0.5 / math.sqrt(FFW)), 0.0).astype(BF)

    def hloop(lo, hi):
        def body(i, _):
            hidden(i)
            return 0
        lax.fori_loop(lo, hi, body, 0)

    hloop(0, 3)
    wait_x(0)
    xfwd(1)
    dfwd(1)
    hloop(3, 6)
    wait_x(1)
    xfwd(2)
    dfwd(2)
    hloop(6, 8)
    wait_x(2)
    dfwd(3)
    for s in range(4):
        wait_d(s)

    def part(d, i):
        g = i // 4
        p = jnp.dot(dbuf[0, d], hbuf[i, 0], preferred_element_type=F32)
        p += jnp.dot(dbuf[1, d], hbuf[i, 1], preferred_element_type=F32)
        p += jnp.dot(a2_ref[g, d], pd[i], preferred_element_type=F32)
        return p

    def chunk(j):
        return lax.rem(j + 4 * (1 - yh), 8)

    znd = at(x, yh, c, zn, yl)
    d0 = lax.rem(z - sgn + 8, 8)

    def first(j, _):
        i = chunk(j)
        snd[i] = part(d0, i).astype(BF)
        rcopy(snd.at[i], rcv.at[0, i], rs_s.at[0, i], rs_r.at[0, i], znd).start()
        return 0

    lax.fori_loop(0, 8, first, 0)

    def middle(n, _):
        s, j = n // 8 + 1, lax.rem(n, 8)
        i = chunk(j)
        d = lax.rem(z - sgn * (1 + s) + 16, 8)
        p = part(d, i)
        rcopy(snd.at[i], rcv.at[s - 1, i], rs_s.at[s - 1, i], rs_r.at[s - 1, i], znd).wait_recv()
        rcv[s - 1, i] = (p + rcv[s - 1, i].astype(F32)).astype(BF)
        rcopy(rcv.at[s - 1, i], rcv.at[s, i], rs_s.at[s, i], rs_r.at[s, i], znd).start()
        return 0

    lax.fori_loop(0, 48, middle, 0)

    def last(j):
        i = chunk(j)
        p = part(z, i)
        rcopy(snd.at[i], rcv.at[6, i], rs_s.at[6, i], rs_r.at[6, i], znd).wait_recv()
        return (p + rcv[6, i].astype(F32)).astype(BF)

    def last_far(j, _):
        fsnd[j] = last(j)
        rcopy(fsnd.at[j], fin.at[yh, j], fs_s.at[j], fs_r.at[j], ypart).start()
        return 0

    lax.fori_loop(0, 4, last_far, 0)

    def last_near(j, _):
        fin[yh, j] = last(j + 4)
        return 0

    lax.fori_loop(0, 4, last_near, 0)

    def finish(j, _):
        rcopy(fsnd.at[j], fin.at[1 - yh, j], fs_s.at[j], fs_r.at[j], ypart).wait()
        w = jnp.concatenate([fin[0, j], fin[1, j]], axis=0).astype(F32)
        for m in range(2):
            out_ref[2 * j + m] = w[:, 128 * m : 128 * (m + 1)].T.astype(BF)
        return 0

    lax.fori_loop(0, 4, finish, 0)

    for h in range(2):
        @pl.when(jnp.logical_not(me_y[h]))
        def _():
            rcopy(dt_ref.at[h], dbuf.at[yl, 2 * x + yh], ys.at[h], yr.at[yh], ypeers[h]).wait_send()
    for s in range(3):
        rcopy(blk(c, 0), blk(c, 0), xs_s.at[s], xs_r.at[s], at(xn, yh, c, z, yl)).wait_send()
    for s in range(4):
        rcopy(blk(c, 0), blk(c, 0), ds_s.at[s], ds_r.at[s], partner).wait_send()

    def drain(n, _):
        s, i = n // 8, lax.rem(n, 8)
        rcopy(snd.at[i], rcv.at[s, i], rs_s.at[s, i], rs_r.at[s, i], znd).wait_send()
        return 0

    lax.fori_loop(0, 56, drain, 0)


def call_k1(dt, base, f, pt, a2):
    v = pl.BlockSpec(memory_space=pltpu.VMEM)
    dma = pltpu.SemaphoreType.DMA
    return pl.pallas_call(
        k1,
        out_shape=jax.ShapeDtypeStruct((8, 128, 320), BF),
        in_specs=[pl.BlockSpec(memory_space=pl.ANY), v, v, v, v],
        out_specs=v,
        scratch_shapes=[
            pltpu.VMEM((2, 8, 160, FP), BF),
            pltpu.VMEM((8, 2, FP, 256), BF),
            pltpu.VMEM((8, 32, 256), BF),
            pltpu.VMEM((8, 160, 256), BF),
            pltpu.VMEM((7, 8, 160, 256), BF),
            pltpu.VMEM((2, 4, 160, 256), BF),
            pltpu.VMEM((4, 160, 256), BF),
            pltpu.VMEM((2, 2, 2, FP, 32), BF),
            dma((2,)), dma((2,)), dma(()), dma((3,)), dma((3,)), dma((4,)), dma((4,)),
            dma((7, 8)), dma((7, 8)), dma((4,)), dma((4,)),
        ],
        compiler_params=pltpu.CompilerParams(
            collective_id=0, has_side_effects=True, vmem_limit_bytes=56 << 20
        ),
        name="k1",
    )(dt, base, f, pt, a2)


def shards(prompt_acts, gate_weight, up_weight, down_weight, d_table, f_table, seeds, fitness):
    yh, yl = lax.axis_index("yh"), lax.axis_index("yl")
    d_sel = jnp.take(d_table, seeds, axis=0, mode="clip")
    f_sel = jnp.take(f_table, seeds, axis=0, mode="clip")
    both = jnp.concatenate([gate_weight, up_weight], axis=1)
    base = lax.psum(jnp.dot(prompt_acts, both, preferred_element_type=F32), MEMBER).astype(BF)
    base = jnp.pad(base.reshape(128, 2, FB), ((0, 0), (0, 0), (0, FP - FB)))
    base = lax.all_gather(base.transpose(1, 2, 0), "yl")
    prompt_full = lax.all_gather(prompt_acts, MEMBER, axis=1, tiled=True)
    dk = d_sel.transpose(1, 0, 2, 3).reshape(3, 32, D)
    proj = jnp.einsum("pd,krd->krp", prompt_full, dk[:2], preferred_element_type=F32)
    pt = lax.all_gather((proj / math.sqrt(D)).astype(BF) * BF(0.5), "yh")
    fk = jnp.pad(f_sel.transpose(1, 0, 2, 3).reshape(3, 32, FB), ((0, 0), (0, 0), (0, FP - FB)))
    f = lax.all_gather(lax.all_gather(fk, "yl"), "yh")
    a2 = dk[2].reshape(32, 8, 2, 2, 160).transpose(2, 3, 1, 4, 0)
    a2 = lax.all_gather(lax.dynamic_index_in_dim(a2, yl, 0, False), "yh")
    a2 = lax.dynamic_index_in_dim(a2, yh, 1, False)
    dt = jnp.pad(down_weight.T.reshape(2, 160, FB), ((0, 0), (0, 0), (0, FP - FB)))
    outputs = call_k1(dt, base, f, pt, a2)
    f_all = lax.all_gather(fk[:, :, :FB], MEMBER).transpose(1, 0, 2, 3).reshape(3, 512, FB)
    d_all = lax.all_to_all(dk, MEMBER, 2, 0, tiled=True).reshape(16, 3, 32, 320).transpose(1, 0, 2, 3).reshape(3, 512, 320)
    fit = lax.all_gather(fitness, MEMBER, tiled=True)
    mean = jnp.sum(fit) / 128
    spread = jnp.sum((fit - mean) ** 2) / 128
    score = (fit - mean) / jnp.sqrt(spread + 1.0)
    w = (d_all.astype(F32) * jnp.repeat(score, 4)[None, :, None]).astype(BF)
    s = 1.0 / math.sqrt(512)
    dg = (jnp.einsum("ma,mb->ab", w[0], f_all[0], preferred_element_type=F32) * s).astype(BF)
    du = (jnp.einsum("ma,mb->ab", w[1], f_all[1], preferred_element_type=F32) * s).astype(BF)
    dd = (jnp.einsum("ma,mb->ab", f_all[2], w[2], preferred_element_type=F32) * s).astype(BF)
    return outputs, dg, du, dd


def solution(mesh):
    split = Mesh(mesh.devices.reshape(4, 2, 2, 8, 2), AX)
    placed = (
        P(None, MEMBER), P(MEMBER, TENSOR), P(MEMBER, TENSOR), P(TENSOR, MEMBER),
        P(MEMBER, None, None, None), P(MEMBER, None, None, TENSOR), P(MEMBER), P(MEMBER),
    )
    return jax.shard_map(
        shards, mesh=split, in_specs=placed,
        out_specs=(P(MEMBER, None, TENSOR), P(MEMBER, TENSOR), P(MEMBER, TENSOR), P(TENSOR, MEMBER)),
        check_vma=False,
    )
```

time: 371 us -> 339 us (0.914)
  Pallas kernels: 0 us -> 121 us
  waiting for transfers between devices: 102 us -> 0.7 us
  blocking collectives: 24.6 us -> 122 us
  local copies, waits for them, and re-layouts: 123 us -> 53.2 us
  starting transfers between devices: 52.9 us -> 8.5 us
  matrix products: 42.5 us -> 8.7 us
    pallas_call x0 -> x1, Pallas kernels: none -> 121 us  [call_k1(): pl.pallas_call(k1, out_shape=jax.ShapeDtypeStruct((8, 128, 320), BF), in_...]
    psum x0 -> x1, blocking collectives: none -> 76.9 us  [shards(): lax.psum(jnp.dot(prompt_acts, both, preferred_element_type=F32), MEMBER)]
    all_to_all x11 -> x1, waiting for transfers between devices: 61.5 us -> 0.01 us  [shards(): lax.all_to_all(dk, MEMBER, 2, 0, tiled=True).reshape(16, 3, 32, 320)]
    all_gather x0 -> x5, blocking collectives: none -> 44.7 us  [the longest x2 15.6 us: shards(): f = lax.all_gather(lax.all_gather(fk, 'yl'), 'yh')]
    all_to_all x11 -> x1, starting transfers between devices: 52.6 us -> 8.42 us  [shards(): lax.all_to_all(dk, MEMBER, 2, 0, tiled=True).reshape(16, 3, 32, 320)]
    unnamed x5 -> x2, waiting for transfers between devices: 40.8 us -> 0.7 us
    unnamed x38 -> x29, local copies, waits for them, and re-layouts: 57.7 us -> 19 us
    dot_general x10 -> x5, matrix products: 42.5 us -> 8.7 us  [the longest x1 2.99 us: shards(): jnp.dot(prompt_acts, both, preferred_element_type=F32)]
  transfers between devices with their start and end apart: 14 -> 3, of which waited for: 9 -> 0; matrix products, arithmetic and copies ran while one was open for 34% -> 18% of each run, Pallas kernels for 0% -> 36%
where the time goes in v1:
time: 339 us; the launch traced here: 335 us
  blocking collectives  122 us (36%)
  Pallas kernels  121 us (36%)
  local copies, waits for them, and re-layouts  53.2 us (16%)
  between operations  16.3 us (5%)
  matrix products  8.7 us (3%)
  starting transfers between devices  8.5 us (3%)
  other arithmetic  4.9 us (1%)
    pallas_call x1, Pallas kernels, call_k1(): pl.pallas_call(k1, out_shape=jax.ShapeDtypeStruct((8, 128, 320), BF), in_...  121 us
    psum x1, blocking collectives, shards(): lax.psum(jnp.dot(prompt_acts, both, preferred_element_type=F32), MEMBER)  76.9 us
    unnamed x29, local copies, waits for them, and re-layouts  19 us
    all_gather x2, blocking collectives, shards(): f = lax.all_gather(lax.all_gather(fk, 'yl'), 'yh')  15.6 us
    all_gather x1, blocking collectives, shards(): a2 = lax.all_gather(lax.dynamic_index_in_dim(a2, yl, 0, False), 'yh')  12.2 us
    all_gather x1, blocking collectives, shards(): base = lax.all_gather(base.transpose(1, 2, 0), 'yl')  12 us
    reshape x2, local copies, waits for them, and re-layouts, shards(): dk = d_sel.transpose(1, 0, 2, 3).reshape(3, 32, D)  9.4 us
    all_to_all x1, starting transfers between devices, shards(): lax.all_to_all(dk, MEMBER, 2, 0, tiled=True).reshape(16, 3, 32, 320)  8.42 us
  transfers between devices with their start and end apart: 3, of which 0 were waited for; matrix products, arithmetic and copies ran while one was open for 18% of the time, Pallas kernels for 36%

profile of v1, /device:TPU:1, one launch (start us, length us, event | category | flops | bytes accessed | tf_op | source)
XLA Modules:
  0.0 335.3 jit_solution(15855364388623634237)
XLA Ops:
  7.2 0.0 copy-start
  7.2 0.0 all-gather.7.cloned.1.call-start
  7.2 0.7 all-gather.7.cloned.1.call-update
  7.9 0.0 all-gather.9.cloned.1.call-start
  8.0 0.7 pad_clamp_fusion
  8.6 1.7 gather_fusion
  10.3 0.1 copy.22
  10.4 0.8 all_gather.51
  11.1 0.0 all-gather.9.cloned.1.call-update
  11.1 0.0 copy-done
  11.2 1.4 gather_fusion.1
  12.6 1.3 copy.25
  13.9 2.5 reshape.42
  16.3 6.9 %copy.26 = bf16[3,32,5120]{1,0,2:T(4,128)(2,1)} copy(bf16[3,32,5120]{2,1,0:T(8,128)(2,1)} %reshape.42) | data formatting | bytes 1966080 | tf_op jit(solution)/shard_map/reshape | solution.py:268
  23.3 7.8 %reshape.73 = bf16[16,2,15360]{2,1,0:T(2,128)(2,1)} reshape(bf16[5120,3,32]{2,1,0:T(4,128)(2,1)} %bitcast.57) | data formatting | bytes 1966080
  31.1 8.4 %all-to-all-start = ((bf16[16,2,15360]{2,1,0:T(2,128)(2,1)}), bf16[16,2,15360]{2,1,0:T(2,128)(2,1)}, u32[]{:S(2)}, u32[]{:S(2)}) async-start(bf16[16,2,15360]{2,1,0:T(2,128)(2,1)} %reshape.73), calls=%async_computation | async-start | bytes 1966080 | tf_op jit(solution)/shard_map/all_to_all | solution.py:279
  39.5 0.1 slice.46
  39.6 0.0 copy-start.7
  39.7 1.1 slice.45
  40.7 0.7 reshape.41
  41.5 1.4 reshape_squeeze.3
  42.9 0.0 copy-done.7
  42.9 0.0 copy-done.8
  43.0 0.0 copy-start.3
  43.0 3.0 convolution_bitcast_fusion
  46.0 0.0 copy-done.10
  46.0 0.6 dynamic-slice.4
  47.2 0.0 copy-done.9
  47.2 0.2 dynamic-update-slice
  47.5 76.9 %all-reduce.6 = (bf16[128,1728]{0,1:T(8,128)(2,1)}, f32[128]{0:T(128)S(1)}) all-reduce(f32[128,1728]{0,1:T(8,128)} %convolution_bitcast_fusion, f32[128]{0:T(128)S(1)} %dynamic-update-slice), channel_id=1, replica_groups=mesh['x'=4,'yh'=2,'c'=2,'z'=8,'yl'=2] {'x','yh','c'}, use_global_device_ids=true, to_apply=%region_0.1 | all-reduce | flops 221312 | bytes 1328128 | tf_op jit(solution)/shard_map/psum | solution.py:264
  124.4 0.7 reduce_sum.18
  125.7 0.7 multiply_reduce_fusion
  127.1 0.0 copy-done.3
  127.1 0.2 constant_dynamic-slice_fusion
  127.3 0.5 copy.30
  127.9 0.0 copy-done.1
  127.9 0.0 copy-start.4
  127.9 1.1 copy.23
  129.0 1.5 slice.33
  130.5 0.0 copy-done.4
  130.5 0.7 pad.14
  131.2 1.9 pad.12.dt_ref
  133.1 0.1 broadcast_in_dim.10
  133.2 0.1 mul.30
  133.3 0.0 copy-start.6
  133.3 12.2 %all_gather.49 = bf16[2,2,8,160,32]{4,3,2,0,1:T(8,128)(2,1)S(1)} all-gather(bf16[1,2,8,160,32]{4,3,2,0,1:T(8,128)(2,1)S(1)} %bitcast.65), channel_id=1, replica_groups=mesh['x'=4,'yh'=2,'c'=2,'z'=8,'yl'=2] {'yh'}, dimensions={0}, use_global_device_ids=true | all-gather | bytes 491520 | tf_op jit(solution)/shard_map/all_gather | solution.py:274
  145.5 0.0 copy-done.5
  145.5 5.6 %all-gather.1 = bf16[6,32,896]{2,1,0:T(8,128)(2,1)S(1)} all-gather(bf16[3,32,896]{2,1,0:T(8,128)(2,1)S(1)} %copy-done.5), channel_id=3, replica_groups=mesh['x'=4,'yh'=2,'c'=2,'z'=8,'yl'=2] {'yl'}, dimensions={0}, use_global_device_ids=true | all-gather | bytes 516096 | tf_op jit(solution)/shard_map/all_gather | solution.py:272
  151.1 0.9 dynamic-slice_bitcast_fusion.a2_ref
  152.0 10.0 %all-gather.2 = bf16[4,3,32,896]{3,2,1,0:T(8,128)(2,1)} all-gather(bf16[2,3,32,896]{3,2,1,0:T(8,128)(2,1)S(1)} %bitcast.66), channel_id=4, replica_groups=mesh['x'=4,'yh'=2,'c'=2,'z'=8,'yl'=2] {'yh'}, dimensions={0}, use_global_device_ids=true | all-gather | bytes 1032192 | tf_op jit(solution)/shard_map/all_gather | solution.py:272
  162.1 12.0 %all-gather = bf16[4,896,128]{2,1,0:T(8,128)(2,1)} all-gather(bf16[2,896,128]{2,1,0:T(8,128)(2,1)S(1)} %pad_bitcast_fusion), channel_id=2, replica_groups=mesh['x'=4,'yh'=2,'c'=2,'z'=8,'yl'=2] {'yl'}, dimensions={0}, use_global_device_ids=true | all-gather | bytes 1376256 | tf_op jit(solution)/shard_map/all_gather | solution.py:266
  174.0 0.0 all-to-all-done
  174.0 7.5 %reshape.74 = bf16[5120,3,32]{2,1,0:T(4,128)(2,1)} reshape(bf16[16,2,15360]{2,1,0:T(2,128)(2,1)} %all-to-all-done) | data formatting | bytes 1966080
  181.5 7.7 %copy.27 = f32[3,32,16,320]{3,1,2,0:T(8,128)} copy(bf16[3,32,16,320]{1,0,3,2:T(4,128)(2,1)} %bitcast.58) | data formatting | bytes 2949120 | tf_op jit(solution)/shard_map/convert_element_type | solution.py:284
  189.2 2.9 fusion
  192.2 1.7 fusion.15
  193.8 4.9 %all-gather.3 = bf16[4,32,128]{2,1,0:T(8,128)(2,1)} all-gather(bf16[2,32,128]{2,1,0:T(8,128)(2,1)S(1)} %fusion.15), channel_id=5, replica_groups=mesh['x'=4,'yh'=2,'c'=2,'z'=8,'yl'=2] {'yh'}, dimensions={0}, use_global_device_ids=true | all-gather | bytes 49152 | tf_op jit(solution)/shard_map/all_gather | solution.py:270
  198.7 121.4 %k1.1 = bf16[8,128,320]{2,1,0:T(8,128)(2,1)} custom-call(bf16[2,160,896]{2,1,0:T(8,128)(2,1)} %pad.12.dt_ref, bf16[2,2,896,128]{3,2,1,0:T(8,128)(2,1)} %bitcast.62, bf16[2,2,3,32,896]{4,3,2,1,0:T(8,128)(2,1)} %bitcast.63, bf16[2,2,32,128]{3,2,1,0:T(8,128)(2,1)} %bitcast.73, bf16[2,8,160,32]{3,2,1,0:T(8,128)(2,1)} %dynamic-slice_bitcast_fusion.a2_ref), custom_call_target="tpu_custom_call" | custom-call | tf_op jit(solution)/shard_map/k1/pallas_call | solution.py:235
  320.1 2.2 copy.29
  322.3 2.1 fusion.19
  324.4 0.0 copy-done.2
  324.4 1.3 fusion.1
  325.8 1.3 fusion.2
  327.1 1.4 fusion.3
  (12 shorter events, 0.1 us)
Async XLA Ops:
  7.2 4.0 %copy-start = (bf16[16,3,4,5120]{3,2,1,0:T(4,128)(2,1)S(1)}, bf16[16,3,4,5120]{3,2,1,0:T(4,128)(2,1)}, u32[]{:S(2)}) copy-start(bf16[16,3,4,5120]{3,2,1,0:T(4,128)(2,1)} %param.12) | copy-start | bytes 5898244
  7.2 185.0 %all-gather.7.cloned.1.call-start = ((), (), s32[]{:S(2)}) async-start(), calls=%async_computation.1 | async-start | bytes 1392640 | tf_op jit(solution)/shard_map/all_gather | solution.py:267
  7.9 314.4 %all-gather.9.cloned.1.call-start = ((), (), s32[]{:S(2)}) async-start(), calls=%async_computation.2 | async-start | bytes 2924544 | tf_op jit(solution)/shard_map/all_gather | solution.py:278
  31.1 143.0 %all-to-all-start = ((bf16[16,2,15360]{2,1,0:T(2,128)(2,1)}), bf16[16,2,15360]{2,1,0:T(2,128)(2,1)}, u32[]{:S(2)}, u32[]{:S(2)}) async-start(bf16[16,2,15360]{2,1,0:T(2,128)(2,1)} %reshape.73), calls=%async_computation | async-start | bytes 1966080 | tf_op jit(solution)/shard_map/all_to_all | solution.py:279
  39.6 3.3 copy-start.7
  40.7 2.2 copy-start.8
  42.9 3.0 copy-start.10
  42.9 4.3 %copy-start.9 = (f32[8]{0:T(128)S(1)}, f32[8]{0:T(128)}, u32[]{:S(2)}) copy-start(f32[8]{0:T(128)} %param.15) | copy-start | bytes 100
  43.0 84.2 %copy-start.3 = (bf16[32,8,2,2,160]{4,3,2,1,0:T(2,128)(2,1)S(1)}, bf16[32,8,2,2,160]{4,3,2,1,0:T(2,128)(2,1)}, u32[]{:S(2)}) copy-start(bf16[32,8,2,2,160]{4,3,2,1,0:T(2,128)(2,1)} %reshape_squeeze.3) | copy-start | bytes 983044
  46.0 81.9 %copy-start.1 = (bf16[2,8,4,5120]{3,2,0,1:T(4,128)(2,1)S(1)}, bf16[2,8,4,5120]{3,2,0,1:T(4,128)(2,1)}, u32[]{:S(2)}) copy-start(bf16[2,8,4,5120]{3,2,0,1:T(4,128)(2,1)} %slice.45) | copy-start | bytes 1966084
  127.9 2.6 copy-start.4
  133.1 12.4 %copy-start.5 = (bf16[3,32,896]{2,1,0:T(8,128)(2,1)S(1)}, bf16[3,32,896]{2,1,0:T(8,128)(2,1)}, u32[]{:S(2)}) copy-start(bf16[3,32,896]{2,1,0:T(8,128)(2,1)} %pad.14) | copy-start | bytes 516100
  133.3 17.8 %copy-start.6 = (bf16[128,1728]{0,1:T(8,128)(2,1)S(1)}, bf16[128,1728]{0,1:T(8,128)(2,1)}, u32[]{:S(2)}) copy-start(bf16[128,1728]{0,1:T(8,128)(2,1)} %get-tuple-element.16) | copy-start | bytes 1327108
  322.3 2.1 copy-start.2
Sparse Core Ops, SparseCore 0:
  10.7 58.0 all-gather.6
  71.4 57.1 all-gather.8

commit v2 on v1

v2 whole, which is shorter than its diff:
```python
import functools
import math

import jax
import jax.numpy as jnp
from jax import lax
from jax.experimental import pallas as pl
from jax.experimental.pallas import tpu as pltpu
from jax.sharding import Mesh
from jax.sharding import PartitionSpec as P

D = 5120
FFW = 13824
FB = 864
AX = ("x", "yh", "c", "z", "yl")
MEMBER = ("x", "yh", "c")
TENSOR = ("z", "yl")
MESH = pl.DeviceIdType.MESH
BF = jnp.bfloat16
F32 = jnp.float32


def rem(a, n):
    return lax.rem(a, n)


def at(x, yh, c, z, yl):
    return {"x": x, "yh": yh, "c": c, "z": z, "yl": yl}


def tn(a, b):
    return lax.dot_general(a, b, (((0,), (0,)), ((), ())), preferred_element_type=F32)


def nt(a, b):
    return lax.dot_general(a, b, (((1,), (1,)), ((), ())), preferred_element_type=F32)


def nn(a, b):
    return jnp.dot(a, b, preferred_element_type=F32)


def step_kernel(
    pt_hbm, gw_hbm, uw_hbm, dt_hbm, dtab_hbm, ftab_hbm, seeds, fit,
    out_ref, dg_ref, du_ref, dd_ref,
    pt_v, w_v, dtab, ftab, dk, fall, foth, dbuf, hbuf, snd, rcv, fin, fsnd, ft,
    bsend, brecv, bown, ps, rsb, basebuf, basef, psh, prb, pjs, pjb, ptt,
    pdc, pdb, dall, fitall, score, wt, a2t,
    in_s, bx_s, bx_r, r1_s, r1_r, ag_s, ag_r, bf_s, bf_r, pr_s, pr_r, pj_s, pj_r,
    ft_s, ft_r, ys, yr, yloc, xo_s, xf_s, x_r, ds_s, ds_r, rs_s, rs_r, fs_s, fs_r,
    pd_s, pd_r, f_s, f_r, ff_s, ff_r, d_s, d_r, q_s, q_r,
):
    x, yh, c, z, yl = [lax.axis_index(a) for a in AX]
    y = 2 * yh + yl
    p = 2 * x + yh
    me = at(x, yh, c, z, yl)
    partner = at(x, yh, 1 - c, z, yl)
    ypart = at(x, 1 - yh, c, z, yl)
    pending = []

    def rc(src, dst, ss, rs, dev):
        return pltpu.make_async_remote_copy(
            src_ref=src, dst_ref=dst, send_sem=ss, recv_sem=rs, device_id=dev, device_id_type=MESH
        )

    def send(src, dst, ss, rs, dev):
        d = rc(src, dst, ss, rs, dev)
        d.start()
        pending.append(d.wait_send)

    def recv(dst, rs):
        rc(dst, dst, rs, rs, partner).wait_recv()

    loads = [
        (gw_hbm, w_v.at[0]), (uw_hbm, w_v.at[1]), (pt_hbm, pt_v), (ftab_hbm, ftab), (dtab_hbm, dtab),
    ]
    loads = [pltpu.make_async_copy(a, b, in_s.at[i]) for i, (a, b) in enumerate(loads)]
    for l in loads:
        l.start()

    def plane(rel):
        ny = rem(y + rel % 4, 4)
        return at(rem(x + rel // 4, 4), ny // 2, c, z, rem(ny, 2))

    def mate(rel):
        q = rem(p + rel // 2, 8)
        return at(q // 2, rem(q, 2), rem(c + rel % 2, 2), z, yl)

    def column(rel):
        return at(x, rem(yh + rel // 8, 2), c, rem(z + rel % 8, 8), yl)

    ypeers = [at(x, h, yl, z, c) for h in range(2)]
    me_y = [(h == yh) & (c == yl) for h in range(2)]
    barrier = pltpu.get_barrier_semaphore()

    def greet(dev):
        pl.semaphore_signal(barrier, inc=1, device_id=dev, device_id_type=MESH)

    peers = [plane(r) for r in range(1, 16)] + [mate(r) for r in range(1, 16, 2)]
    peers += [column(r) for r in range(1, 16) if r != 8]
    for o in peers:
        greet(o)
    for h in range(2):
        @pl.when(c != yl)
        def _():
            greet(ypeers[h])

    for l in loads[:3]:
        l.wait()

    def partial_base(k):
        return tn(w_v[k], pt_v[...])

    bsend[pl.ds(0, FB)] = partial_base(1 - c).astype(BF)
    bsend[pl.ds(FB, 32)] = jnp.zeros((32, 128), BF)

    n_peers = len(peers)

    @pl.when(c == yl)
    def _():
        pl.semaphore_wait(barrier, n_peers)

    @pl.when(c != yl)
    def _():
        pl.semaphore_wait(barrier, n_peers + 2)

    send(bsend, brecv, bx_s, bx_r, partner)

    for h in range(2):
        @pl.when(jnp.logical_not(me_y[h]))
        def _():
            rc(dt_hbm.at[h], dbuf.at[yl, 2 * x + yh], ys.at[h], yr.at[yh], ypeers[h]).start()
        @pl.when(me_y[h])
        def _():
            pltpu.make_async_copy(dt_hbm.at[h], dbuf.at[yl, 2 * x + yh], yloc).start()

    def wait_y():
        for h in range(2):
            @pl.when(jnp.logical_not(me_y[h]))
            def _():
                rc(dt_hbm.at[h], dbuf.at[c, 2 * x + h], ys.at[h], yr.at[h], ypeers[h]).wait_recv()
                rc(dt_hbm.at[h], dbuf.at[c, 2 * x + h], ys.at[h], yr.at[h], ypeers[h]).wait_send()
            @pl.when(me_y[h])
            def _():
                pltpu.make_async_copy(dt_hbm.at[h], dbuf.at[yl, 2 * x + yh], yloc).wait()

    ptr = pt_v[...].astype(F32).T.astype(BF)
    psh[...] = jnp.zeros_like(psh)

    @pl.when(c == 0)
    def _():
        psh[:, 0:320] = ptr

    @pl.when(c == 1)
    def _():
        psh[:, 64:384] = ptr

    toks = pl.ds(pl.multiple_of(16 * z, 16), 16)
    for r in range(1, 16):
        send(psh.at[toks], prb.at[r], pr_s.at[r], pr_r.at[r], mate(r))

    bown[pl.ds(0, FB)] = partial_base(c)
    bown[pl.ds(FB, 32)] = jnp.zeros((32, 128), F32)
    recv(brecv, bx_r)
    for q in range(8):
        rows = pl.ds(112 * q, 112)
        ps[q] = (bown[rows] + brecv[rows].astype(F32)).astype(BF)
    for r in range(1, 8):
        q = rem(p + r, 8)
        send(ps.at[q], rsb.at[r], r1_s.at[r], r1_r.at[r], at(q // 2, rem(q, 2), c, z, yl))

    loads[3].wait()
    for k in range(3):
        for m in range(8):
            fall[k, c, p, pl.ds(4 * m, 4)] = ftab[seeds[m], k]
    fteam = [(1, 0), (0, 1), (1, 1)]
    for i, (dh, dl) in enumerate(fteam):
        dev = at(x, rem(yh + dh, 2), c, z, rem(yl + dl, 2))
        dst = fall.at[:, c, p] if dl == 0 else foth.at[yh]
        send(fall.at[:, c, p], dst, ft_s.at[i], ft_r.at[i], dev)

    loads[4].wait()
    for k in range(3):
        for m in range(8):
            dk[k, pl.ds(4 * m, 4)] = dtab[seeds[m], k]

    def proj_of(r, piece):
        q = rem(p - r // 2 + 8, 8)
        cc = rem(c + r % 2, 2)
        lanes = pl.ds(pl.multiple_of(640 * q + 256 * cc, 128), 384)
        return nt(piece, dk[0:2, :, lanes].reshape(64, 384))

    acc = proj_of(0, psh[toks])
    for r in range(1, 16):
        recv(prb.at[r], pr_r.at[r])
        acc += proj_of(r, prb[r])
    acc = (acc / math.sqrt(D)).astype(BF).astype(F32)
    kk = lax.broadcasted_iota(jnp.int32, (16, 64), 1) // 32
    acc = jnp.where(kk == 0, acc * 0.25, acc * 0.5)
    pjs[...] = jnp.zeros_like(pjs)
    pjs[:, 0:64] = acc.astype(BF)
    for r in range(1, 16):
        send(pjs, pjb.at[yh, toks], pj_s.at[r], pj_r.at[r], column(r))
    pjb[yh, toks] = pjs[...]

    s = bown[pl.ds(pl.multiple_of(112 * p, 16), 112)] + brecv[pl.ds(pl.multiple_of(112 * p, 16), 112)].astype(F32)
    for r in range(1, 8):
        recv(rsb.at[r], r1_r.at[r])
        s += rsb[r].astype(F32)

    def brows(q):
        return pl.ds(pl.multiple_of(112 * q, 16), 112)

    basebuf[yl, c, brows(p)] = s.astype(BF)
    for r in range(1, 16):
        send(basebuf.at[yl, c, brows(p)], basebuf.at[yl, c, brows(p)], ag_s.at[r], ag_r.at[r], plane(r))

    e, kz = rem(z, 2), z // 2

    def zblk(r, ab):
        x0 = rem(x - r + 4, 4)
        m = rem(x0 - kz + 4, 4)
        low = jnp.where(e == 0, jnp.where(m == 1, 0, 1), jnp.where(m == 3, 1, 0))
        return 2 * x0 + (low if ab == 0 else 1 - low)

    xnb = [at(rem(x + 1, 4), yh, c, z, yl), at(rem(x + 3, 4), yh, c, z, yl)]

    def dsend(r, ab):
        b = zblk(r, ab)
        send(dbuf.at[c, b], dbuf.at[c, b], ds_s.at[r, ab], ds_r.at[r, ab], partner)

    def own_x(ab):
        b = dbuf.at[c, zblk(0, ab)]
        send(b, b, xo_s.at[0, ab], x_r.at[1, ab], xnb[0])
        send(b, b, xo_s.at[1, ab], x_r.at[3, ab], xnb[1])
        dsend(0, ab)

    def take_x(r, ab):
        b = dbuf.at[c, zblk(r, ab)]
        recv(b, x_r.at[r, ab])
        if r != 2:
            fwd = c == (0 if r == 1 else 1)
            d = rc(b, b, xf_s.at[r, ab], x_r.at[2, ab], xnb[0 if r == 1 else 1])
            pl.when(fwd)(d.start)
            pending.append(lambda: pl.when(fwd)(d.wait_send))
        dsend(r, ab)

    def take_d(r, ab):
        recv(dbuf.at[1 - c, zblk(r, ab)], ds_r.at[r, ab])

    wait_y()
    own_x(0)

    for i, (dh, dl) in enumerate(fteam):
        if dl == 0:
            recv(fall.at[:, c, p + 1 - 2 * yh], ft_r.at[i])
        else:
            recv(foth.at[rem(yh + dh, 2)], ft_r.at[i])

    def fac(g, tau):
        return fall.at[:, c, 2 * x + g] if tau == 0 else foth.at[g]

    for g in range(2):
        for tau in range(2):
            for k in range(2):
                ft[g, tau, k] = fac(g, tau)[k].T
    for r in range(1, 16):
        hz, zz = rem(yh + r // 8, 2), rem(z - r % 8 + 8, 8)
        recv(pjb.at[hz, pl.ds(pl.multiple_of(16 * zz, 16), 16)], pj_r.at[r])
    for g in range(2):
        ptt[g] = pjb[g].astype(F32).T[0:64].reshape(2, 32, 128)

    for r in range(1, 16):
        xx, yy = rem(x - r // 4 + 4, 4), rem(y - r % 4 + 4, 4)
        piece = basebuf.at[rem(yy, 2), c, brows(2 * xx + yy // 2)]
        recv(piece, ag_r.at[r])
    send(basebuf.at[:, c], basebuf.at[:, c], bf_s, bf_r, partner)

    take_x(1, 0)
    take_x(3, 0)
    own_x(1)
    recv(basebuf.at[:, 1 - c], bf_r)
    for tau in range(2):
        t = rem(yl + tau, 2)
        for k in range(2):
            b = basebuf[t, k, pl.ds(0, FB)].astype(F32)
            basef[tau, k] = b * 0.5 if k == 0 else b
    take_x(2, 0)
    for r in range(4):
        take_d(r, 0)

    rowm = lax.broadcasted_iota(jnp.int32, (32, 256), 0) // 4
    lanem = lax.broadcasted_iota(jnp.int32, (32, 256), 1) // 128

    def hidden(i):
        g, cc = i // 4, rem(i, 4)
        live = rowm == 2 * cc + lanem
        pm = [
            jnp.where(live, jnp.concatenate([ptt[g, k]] * 2, axis=1), 0.0).astype(BF)
            for k in range(2)
        ]
        for tau in range(2):
            def rows(rb, _):
                r = pl.ds(pl.multiple_of(rb * 48, 16), 48)
                b = [basef[tau, k, r] for k in range(2)]
                gu = [
                    jnp.concatenate([b[k], b[k]], axis=1) + nn(ft[g, tau, k, r], pm[k])
                    for k in range(2)
                ]
                hbuf[i, tau, r] = ((gu[0] + gu[0] * jnp.tanh(gu[0])) * gu[1]).astype(BF)
                return 0
            lax.fori_loop(0, 18, rows, 0, unroll=3)

    def chunk(j):
        return rem(j + 4 * (1 - yh), 8)

    sgn = 1 - 2 * c
    zn = rem(z + sgn + 8, 8)
    znd = at(x, yh, c, zn, yl)

    def part(d, i):
        return nn(dbuf[yl, d], hbuf[i, 0]) + nn(dbuf[1 - yl, d], hbuf[i, 1])

    d0 = rem(z - sgn + 8, 8)

    def first(j, _):
        i = chunk(j)
        hidden(i)
        snd[i] = part(d0, i).astype(BF)
        rc(snd.at[i], rcv.at[0, i], rs_s.at[0, i], rs_r.at[0, i], znd).start()
        return 0

    lax.fori_loop(0, 8, first, 0)

    tot = jnp.zeros((32, 128), F32)
    for cc in range(4):
        i = 4 * yh + cc
        q = nn(fall[2, c, p], hbuf[i, 0]) + nn(foth[yh, 2], hbuf[i, 1])
        q = jnp.where(rowm == 2 * cc + lanem, q, 0.0)
        tot += q[:, :128] + q[:, 128:]
    pdc[...] = tot
    for r in range(1, 8):
        send(pdc, pdb.at[r], pd_s.at[r], pd_r.at[r], column(r))

    take_x(1, 1)
    take_x(3, 1)
    take_x(2, 1)
    for r in range(4):
        take_d(r, 1)

    for i in range(1, 8):
        q = rem(p + i, 8)
        far = q != (p + 1 - 2 * yh)
        d = rc(fall.at[:, c, p], fall.at[:, c, p], f_s.at[i], f_r.at[i], at(q // 2, rem(q, 2), c, z, yl))
        pl.when(far)(d.start)
        pending.append(functools.partial(pl.when(far), d.wait_send))
    for m in range(8):
        fitall[c, p, pl.ds(4 * m, 4)] = jnp.full((4, 128), fit[m], F32)

    def dlanes(q, cc):
        return pl.ds(pl.multiple_of(640 * q + 256 * cc, 128), 384)

    dall[:, c, p] = dk[:, :, dlanes(p, c)]
    for r in range(1, 16):
        q, cc = rem(p + r // 2, 8), rem(c + r % 2, 2)
        send(dk.at[:, :, dlanes(q, cc)], dall.at[:, c, p], d_s.at[r], d_r.at[r], mate(r))
        send(fitall.at[c, p], fitall.at[c, p], q_s.at[r], q_r.at[r], mate(r))

    def middle(n, _):
        s, j = n // 8 + 1, rem(n, 8)
        i = chunk(j)
        pp = part(rem(z - sgn * (1 + s) + 16, 8), i)
        recv(rcv.at[s - 1, i], rs_r.at[s - 1, i])
        rcv[s - 1, i] = (pp + rcv[s - 1, i].astype(F32)).astype(BF)
        rc(rcv.at[s - 1, i], rcv.at[s, i], rs_s.at[s, i], rs_r.at[s, i], znd).start()
        return 0

    lax.fori_loop(0, 32, middle, 0)

    for i in range(1, 8):
        q = rem(p - i + 8, 8)
        far = q != (p + 1 - 2 * yh)
        pl.when(far)(functools.partial(recv, fall.at[:, c, q], f_r.at[i]))
    send(fall.at[:, c], fall.at[:, c], ff_s, ff_r, partner)

    lax.fori_loop(32, 40, middle, 0)

    for r in range(1, 16):
        q, cc = rem(p - r // 2 + 8, 8), rem(c + r % 2, 2)
        recv(dall.at[:, cc, q], d_r.at[r])
        recv(fitall.at[cc, q], q_r.at[r])
    recv(fall.at[:, 1 - c], ff_r)
    fv = fitall[...].reshape(512, 128)
    mean = jnp.sum(fv, axis=0, keepdims=True) / 512
    spread = jnp.sum((fv - mean) ** 2, axis=0, keepdims=True) / 512
    score[...] = ((fv - mean) / jnp.sqrt(spread + 1.0)).reshape(2, 8, 32, 128)
    for k in range(3):
        def weigh(g, _):
            a, b = g // 8, rem(g, 8)
            sc = score[a, b]
            w = dall[k, a, b].astype(F32) * jnp.concatenate([sc] * 3, axis=1)
            dall[k, a, b] = w.astype(BF)
            return 0
        lax.fori_loop(0, 16, weigh, 0)
        wt[k] = dall[k].reshape(512, 384).T

    def deltas(k, ref):
        def rows(rb, _):
            r = pl.ds(pl.multiple_of(64 * c + 32 * rb, 16), 32)
            v = nn(wt[k, r], fall[k].reshape(512, FB)) * (1.0 / math.sqrt(512))
            ref[pl.ds(pl.multiple_of(32 * rb, 16), 32)] = v.astype(BF)
            return 0
        lax.fori_loop(0, 10, rows, 0)

    deltas(0, dg_ref)
    deltas(1, du_ref)
    deltas(2, dd_ref)

    lax.fori_loop(40, 48, middle, 0)

    tot = pdc[...]
    for r in range(1, 8):
        recv(pdb.at[r], pd_r.at[r])
        tot += pdb[r]
    tot = (tot / math.sqrt(FFW)).astype(BF).astype(F32) * 0.5
    pdc2 = tot
    a2t[...] = dk[2, :, pl.ds(pl.multiple_of(640 * z + 256 * yl, 128), 384)].T
    pdb[0] = pdc2

    def last(j):
        i = chunk(j)
        pp = part(z, i)
        recv(rcv.at[6, i], rs_r.at[6, i])
        return (pp + rcv[6, i].astype(F32)).astype(BF)

    def last_far(j, _):
        fsnd[j] = last(j)
        rc(fsnd.at[j], fin.at[yh, j], fs_s.at[j], fs_r.at[j], ypart).start()
        return 0

    lax.fori_loop(0, 4, last_far, 0)

    def last_near(j, _):
        fin[yh, j] = last(j + 4)
        return 0

    lax.fori_loop(0, 4, last_near, 0)

    def finish(j, _):
        rc(fsnd.at[j], fin.at[1 - yh, j], fs_s.at[j], fs_r.at[j], ypart).wait()
        live = rowm == 2 * j + lanem
        pm = jnp.where(live, jnp.concatenate([pdb[0]] * 2, axis=1), 0.0).astype(BF)
        for h in range(2):
            r = pl.ds(pl.multiple_of(64 * yl + 160 * h, 16), 160)
            w = (fin[h, j].astype(F32) + nn(a2t[r], pm)).astype(BF)
            for m in range(2):
                out_ref[2 * j + m, pl.ds(160 * h, 160)] = w[:, 128 * m : 128 * (m + 1)]
        return 0

    lax.fori_loop(0, 4, finish, 0)

    for w in pending:
        w()

    def drain(n, _):
        s, i = n // 8, rem(n, 8)
        rc(snd.at[i], rcv.at[s, i], rs_s.at[s, i], rs_r.at[s, i], znd).wait_send()
        return 0

    lax.fori_loop(0, 56, drain, 0)


def call_step(pt, gw, uw, dt, dtab, ftab, seeds, fit):
    v = pl.BlockSpec(memory_space=pltpu.VMEM)
    a = pl.BlockSpec(memory_space=pl.ANY)
    sm = pl.BlockSpec(memory_space=pltpu.SMEM)
    dma = pltpu.SemaphoreType.DMA
    vm = pltpu.VMEM
    return pl.pallas_call(
        step_kernel,
        out_shape=[
            jax.ShapeDtypeStruct((8, 320, 128), BF),
            jax.ShapeDtypeStruct((320, FB), BF),
            jax.ShapeDtypeStruct((320, FB), BF),
            jax.ShapeDtypeStruct((320, FB), BF),
        ],
        in_specs=[a, a, a, a, a, a, sm, sm],
        out_specs=[v, v, v, v],
        scratch_shapes=[
            vm((320, 128), BF), vm((2, 320, FB), BF), vm((16, 3, 4, D), BF), vm((16, 3, 4, FB), BF),
            vm((3, 32, D), BF), vm((3, 2, 8, 32, FB), BF), vm((2, 3, 32, FB), BF),
            vm((2, 8, 160, FB), BF), vm((8, 2, FB, 256), BF), vm((8, 160, 256), BF),
            vm((7, 8, 160, 256), BF), vm((2, 4, 160, 256), BF), vm((4, 160, 256), BF),
            vm((2, 2, 2, FB, 32), BF),
            vm((896, 128), BF), vm((896, 128), BF), vm((896, 128), F32), vm((8, 112, 128), BF),
            vm((8, 112, 128), BF), vm((2, 2, 896, 128), BF), vm((2, 2, FB, 128), F32),
            vm((128, 384), BF), vm((16, 16, 384), BF), vm((16, 128), BF), vm((2, 128, 128), BF),
            vm((2, 2, 32, 128), F32),
            vm((32, 128), F32), vm((8, 32, 128), F32), vm((3, 2, 8, 32, 384), BF),
            vm((2, 8, 32, 128), F32), vm((2, 8, 32, 128), F32), vm((3, 384, 512), BF), vm((384, 32), BF),
            dma((5,)), dma(()), dma(()), dma((8,)), dma((8,)), dma((16,)), dma((16,)), dma(()), dma(()),
            dma((16,)), dma((16,)), dma((16,)), dma((16,)),
            dma((3,)), dma((3,)), dma((2,)), dma((2,)), dma(()), dma((2, 2)), dma((4, 2)), dma((4, 2)),
            dma((4, 2)), dma((4, 2)), dma((7, 8)), dma((7, 8)), dma((4,)), dma((4,)),
            dma((8,)), dma((8,)), dma((8,)), dma((8,)), dma(()), dma(()), dma((16,)), dma((16,)),
            dma((16,)), dma((16,)),
        ],
        compiler_params=pltpu.CompilerParams(
            collective_id=0, has_side_effects=True, vmem_limit_bytes=60 << 20
        ),
        name="es_step",
    )(pt, gw, uw, dt, dtab, ftab, seeds, fit)


def shards(prompt_acts, gate_weight, up_weight, down_weight, d_table, f_table, seeds, fitness):
    out, dg, du, dd = call_step(
        prompt_acts.T, gate_weight, up_weight, down_weight.T.reshape(2, 160, FB), d_table, f_table,
        seeds, fitness,
    )
    return out.transpose(0, 2, 1), dg, du, dd.T


def solution(mesh):
    split = Mesh(mesh.devices.reshape(4, 2, 2, 8, 2), AX)
    placed = (
        P(None, MEMBER), P(MEMBER, TENSOR), P(MEMBER, TENSOR), P(TENSOR, MEMBER),
        P(MEMBER, None, None, None), P(MEMBER, None, None, TENSOR), P(MEMBER), P(MEMBER),
    )
    return jax.shard_map(
        shards, mesh=split, in_specs=placed,
        out_specs=(P(MEMBER, None, TENSOR), P(MEMBER, TENSOR), P(MEMBER, TENSOR), P(TENSOR, MEMBER)),
        check_vma=False,
    )
```

time: 339 us -> 152 us (0.45)
  the two profiles are of different devices: /device:TPU:1 before, /device:TPU:8 now
where the time goes in v2:
time: 152 us; the launch traced here: 151 us
  Pallas kernels  145 us (95%)
  local copies, waits for them, and re-layouts  5.6 us (4%)
    pallas_call x1, Pallas kernels, call_step(): pl.pallas_call(step_kernel, out_shape=[jax.ShapeDtypeStruct((8, 320, 128)...  145 us
    unnamed x8, local copies, waits for them, and re-layouts  5.6 us

profile of v2, /device:TPU:8, one launch (start us, length us, event | category | flops | bytes accessed | tf_op | source)
XLA Modules:
  0.0 151.4 jit_solution(10792257954056515269)
XLA Ops:
  0.6 145.1 %es_step.1 = (bf16[8,320,128]{2,1,0:T(8,128)(2,1)}, bf16[320,864]{1,0:T(8,128)(2,1)}, bf16[320,864]{1,0:T(8,128)(2,1)}, bf16[320,864]{1,0:T(8,128)(2,1)}) custom-call(bf16[320,128]{1,0:T(8,128)(2,1)} %bitcast.9, bf16[320,864]{1,0:T(8,128)(2,1)} %gw_hbm.1, bf16[320,864]{1,0:T(8,128)(2,1)} %uw_hbm.1, bf16[2,160,864]{2,1,0:T(8,128)(2,1)} %bitcast.7, ...), custom_call_target="tpu_custom_call" | custom-call | tf_op jit(solution)/shard_map/es_step/pallas_call | solution.py:479
  145.7 0.0 copy-start.1
  145.7 0.0 copy-start
  145.8 2.1 %copy.16 = bf16[8,128,320]{1,2,0:T(8,128)(2,1)} copy(bf16[8,128,320]{1,2,0:T(8,128)(2,1)} %bitcast.6) | data formatting | bytes 1310720
  147.8 1.9 %copy.17 = bf16[320,864]{1,0:T(8,128)(2,1)} copy(bf16[320,864]{1,0:T(8,128)(2,1)} %get-tuple-element.17) | data formatting | bytes 1105920
  149.7 0.0 copy-done.1
  149.7 0.8 copy.18
  150.5 0.0 copy-done
  150.6 0.8 copy.19
Async XLA Ops:
  145.7 4.0 %copy-start.1 = (bf16[320,864]{1,0:T(8,128)(2,1)S(1)}, bf16[320,864]{1,0:T(8,128)(2,1)}, u32[]{:S(2)}) copy-start(bf16[320,864]{1,0:T(8,128)(2,1)} %get-tuple-element.18) | copy-start | bytes 1658884
  145.7 4.8 %copy-start = (bf16[320,864]{1,0:T(8,128)(2,1)S(1)}, bf16[320,864]{1,0:T(8,128)(2,1)}, u32[]{:S(2)}) copy-start(bf16[320,864]{1,0:T(8,128)(2,1)} %get-tuple-element.11) | copy-start | bytes 1658884

commit v3 on v2

v3 whole, which is shorter than its diff:
```python
import functools
import math

import jax
import jax.numpy as jnp
from jax import lax
from jax.experimental import pallas as pl
from jax.experimental.pallas import tpu as pltpu
from jax.sharding import Mesh
from jax.sharding import PartitionSpec as P

D = 5120
FFW = 13824
FB = 864
AX = ("x", "yh", "c", "z", "yl")
MEMBER = ("x", "yh", "c")
TENSOR = ("z", "yl")
MESH = pl.DeviceIdType.MESH
BF = jnp.bfloat16
F32 = jnp.float32
HR = 864
HU = 1
LEAD = 4
TB = 0
ORDER = (
    "y_first",
    "y_second",
    "base_half",
    "base_scatter",
    "prompt_out",
    "local_rows",
    "base_sum",
    "factors_far",
    "prompt_on",
    "factors_near",
    "x_first",
    "base_on",
    "project",
    "take_first",
    "x_second",
    "factors_far_in",
    "base_end",
    "project_in",
    "base_other",
    "hidden_ahead",
    "factors_near_in",
    "take_first_far",
)


def rem(a, n):
    return lax.rem(a, n)


def at(x, yh, c, z, yl):
    return {"x": x, "yh": yh, "c": c, "z": z, "yl": yl}


def tn(a, b):
    return lax.dot_general(a, b, (((0,), (0,)), ((), ())), preferred_element_type=F32)


def nt(a, b):
    return lax.dot_general(a, b, (((1,), (1,)), ((), ())), preferred_element_type=F32)


def nn(a, b):
    return jnp.dot(a, b, preferred_element_type=F32)


def step_kernel(
    pt_hbm, gw_hbm, uw_hbm, dt_hbm, dtab_hbm, ftab_hbm, seeds, fit,
    out_ref, del_ref,
    pt_v, w_v, dt_v, dtab, ftab, dk, fall, foth, dbuf, hbuf, snd, rcv, fin, fsnd,
    bsend, brecv, bown, ps, rsb, lhs, rhs, psh, prb, pjs, pjb, ptt,
    pdc, pdb, pdt, dall, fitall, score, wt, a2t, nbuf,
    in_s, bx_s, bx_r, r1_s, r1_r, ag_s, ag_r, ah_s, ah_r, bf_s, bf_r, pr_s, pr_r, pj_s, pj_r,
    ft_s, ft_r, ft2_s, ft2_r, ys, yr, yloc, xo_s, xf_s, x_r, ds_s, ds_r, rs_s, rs_r, fs_s, fs_r,
    pd_s, pd_r, f_s, f_r, ff_s, ff_r, d_s, d_r, q_s, q_r,
):
    x, yh, c, z, yl = [lax.axis_index(a) for a in AX]
    y = 2 * yh + yl
    p = 2 * x + yh
    me = at(x, yh, c, z, yl)
    partner = at(x, yh, 1 - c, z, yl)
    ypart = at(x, 1 - yh, c, z, yl)
    pending = []

    def rc(src, dst, ss, rs, dev):
        return pltpu.make_async_remote_copy(
            src_ref=src, dst_ref=dst, send_sem=ss, recv_sem=rs, device_id=dev, device_id_type=MESH
        )

    def send(src, dst, ss, rs, dev):
        d = rc(src, dst, ss, rs, dev)
        d.start()
        pending.append(d.wait_send)

    def recv(dst, rs):
        rc(dst, dst, rs, rs, partner).wait_recv()

    loads = [
        (gw_hbm, w_v.at[0]), (uw_hbm, w_v.at[1]), (pt_hbm, pt_v), (ftab_hbm, ftab), (dtab_hbm, dtab),
        (dt_hbm, dt_v),
    ]
    loads = [pltpu.make_async_copy(a, b, in_s.at[i]) for i, (a, b) in enumerate(loads)]
    for l in loads:
        l.start()

    def plane(rel):
        ny = rem(y + rel % 4, 4)
        return at(rem(x + rel // 4, 4), ny // 2, c, z, rem(ny, 2))

    def mate(rel):
        q = rem(p + rel // 2, 8)
        return at(q // 2, rem(q, 2), rem(c + rel % 2, 2), z, yl)

    def column(rel):
        return at(x, rem(yh + rel // 8, 2), c, rem(z + rel % 8, 8), yl)

    ypeers = [at(x, h, yl, z, c) for h in range(2)]
    me_y = [(h == yh) & (c == yl) for h in range(2)]
    barrier = pltpu.get_barrier_semaphore()

    def greet(dev):
        pl.semaphore_signal(barrier, inc=1, device_id=dev, device_id_type=MESH)

    peers = [plane(r) for r in range(1, 16)] + [mate(r) for r in range(1, 16, 2)]
    peers += [column(r) for r in range(1, 16) if r != 8]
    for o in peers:
        greet(o)
    for h in range(2):
        @pl.when(c != yl)
        def _():
            greet(ypeers[h])

    for l in loads[:3]:
        l.wait()

    def partial_base(k):
        return tn(w_v[k], pt_v[...])

    bsend[pl.ds(0, FB)] = partial_base(1 - c).astype(BF)
    bsend[pl.ds(FB, 32)] = jnp.zeros((32, 128), BF)
    loads[3].wait()
    for k in range(3):
        for m in range(8):
            fall[k, c, p, pl.ds(4 * m, 4)] = ftab[seeds[m], k]
    loads[5].wait()
    n_peers = len(peers)
    @pl.when(c == yl)
    def _():
        pl.semaphore_wait(barrier, n_peers)

    @pl.when(c != yl)
    def _():
        pl.semaphore_wait(barrier, n_peers + 2)

    e, kz = rem(z, 2), z // 2

    def low(x0):
        m = rem(x0 - kz + 4, 4)
        return jnp.where(e == 0, jnp.where(m == 1, 0, 1), jnp.where(m == 3, 1, 0))

    def zblk(r, ab):
        x0 = rem(x - r + 4, 4)
        return 2 * x0 + (low(x0) if ab == 0 else 1 - low(x0))

    own_a = low(x)

    def ysend(ab):
        mine = yh == (own_a if ab == 0 else 1 - own_a)
        for h in range(2):
            @pl.when(mine & jnp.logical_not(me_y[h]))
            def _():
                rc(dt_v.at[h], dbuf.at[yl, 2 * x + yh], ys.at[h], yr.at[yh], ypeers[h]).start()
            @pl.when(mine & me_y[h])
            def _():
                pltpu.make_async_copy(dt_hbm.at[h], dbuf.at[yl, 2 * x + yh], yloc).start()

    def wait_y(ab):
        w = own_a if ab == 0 else 1 - own_a
        here = (w == yh) & (c == yl)

        @pl.when(jnp.logical_not(here))
        def _():
            recv(dbuf.at[c, 2 * x + w], yr.at[w])

        @pl.when(here)
        def _():
            pltpu.make_async_copy(dt_hbm.at[0], dbuf.at[c, 2 * x + w], yloc).wait()

    def y_drain():
        for h in range(2):
            @pl.when(jnp.logical_not(me_y[h]))
            def _():
                rc(dt_v.at[h], dbuf.at[yl, 2 * x + yh], ys.at[h], yr.at[yh], ypeers[h]).wait_send()

    pending.append(y_drain)
    xnb = [at(rem(x + 1, 4), yh, c, z, yl), at(rem(x + 3, 4), yh, c, z, yl)]

    def dsend(r, ab):
        b = dbuf.at[c, zblk(r, ab)]
        d = rc(b, b, ds_s.at[r, ab], ds_r.at[r, ab], partner)
        pending.append(d.wait_send)
        return d

    def own_x(ab):
        b = dbuf.at[c, zblk(0, ab)]
        send(b, b, xo_s.at[0, ab], x_r.at[1, ab], xnb[0])
        send(b, b, xo_s.at[1, ab], x_r.at[3, ab], xnb[1])
        dsend(0, ab).start()

    def taker(r, ab):
        b = dbuf.at[c, zblk(r, ab)]
        d2 = dsend(r, ab)
        if r == 2:
            def run():
                recv(b, x_r.at[r, ab])
                d2.start()
            return run
        fwd = c == (0 if r == 1 else 1)
        d = rc(b, b, xf_s.at[r, ab], x_r.at[2, ab], xnb[0 if r == 1 else 1])
        pending.append(lambda: pl.when(fwd)(d.wait_send))

        def run():
            recv(b, x_r.at[r, ab])
            pl.when(fwd)(d.start)
            d2.start()

        return run

    take = {(r, ab): taker(r, ab) for r in (1, 3, 2) for ab in range(2)}

    def take_d(r, ab):
        recv(dbuf.at[1 - c, zblk(r, ab)], ds_r.at[r, ab])

    toks = pl.ds(pl.multiple_of(16 * z, 16), 16)
    own_row = 4 * yh + x
    def bpiece(t, k, first, rows):
        return lhs.at[t, k, pl.ds(pl.multiple_of(112 * first, 16), rows), pl.ds(0, 128)]

    along_x = [at(rem(x + r, 4), yh, c, z, yl) for r in range(4)]
    along_y = [at(x, rem(y + r, 4) // 2, c, z, rem(y + r, 2)) for r in range(4)]
    stage1, stage2, got1, got2 = [], [], [], []
    for r in range(1, 4):
        b = bpiece(yl, c, own_row, 112)
        stage1.append((rc(b, b, ag_s.at[r], ag_r.at[r], along_x[r]), rc(b, b, ag_s.at[r], ag_r.at[r], along_y[r])))
        xx, yy = rem(x - r + 4, 4), rem(y - r + 4, 4)
        got1.append((bpiece(yl, c, 4 * yh + xx, 112), bpiece(rem(yy, 2), c, 4 * (yy // 2) + x, 112)))
        b = bpiece(yl, c, 4 * yh, 448)
        far = []
        for n in range(4):
            f = bpiece(n // 2, c, 4 * (n % 2) + x, 112)
            far.append(rc(f, f, ah_s.at[r, n], ah_r.at[r, n], along_x[r]))
        stage2.append(([rc(b, b, ah_s.at[r, 0], ah_r.at[r, 0], along_y[r])], far))
        got2.append((
            [bpiece(rem(yy, 2), c, 4 * (yy // 2), 448)],
            [bpiece(n // 2, c, 4 * (n % 2) + xx, 112) for n in range(4)],
        ))

    def by_core(f):
        for core in range(2):
            @pl.when(c == core)
            def _():
                f(core)

    def ag_one(core):
        for d in stage1:
            d[core].start()

    def ag_two(core):
        for g, r in zip(got1, range(1, 4)):
            recv(g[core], ag_r.at[r])
        for ds in stage2:
            for d in ds[core]:
                d.start()

    def ag_end(core):
        for g, r in zip(got2, range(1, 4)):
            for n, b in enumerate(g[core]):
                recv(b, ah_r.at[r, n])

    def ag_drain(core):
        for d in stage1:
            d[core].wait_send()
        for ds in stage2:
            for d in ds[core]:
                d.wait_send()

    pending.append(lambda: by_core(ag_drain))
    fteam = [(1, 0), (1, 1), (0, 1)]

    def fdev(i):
        dh, dl = fteam[i]
        return at(x, rem(yh + dh, 2), c, z, rem(yl + dl, 2))

    def fdst(i, ks):
        return fall.at[ks, c, p] if fteam[i][1] == 0 else foth.at[yh, ks]

    def frcv(i, ks):
        dh, dl = fteam[i]
        return fall.at[ks, c, p + 1 - 2 * yh] if dl == 0 else foth.at[rem(yh + dh, 2), ks]

    gu, down = pl.ds(0, 2), pl.ds(2, 1)
    def factors_in(own, where):
        for i in where:
            recv(frcv(i, gu), ft_r.at[i])
        g = yh if own else 1 - yh
        for k in range(2):
            lanes = pl.ds(160 if own else 128, 32)
            lhs[yl, k, pl.ds(0, FB), lanes] = fall[k, c, 2 * x + g].T
            lhs[1 - yl, k, pl.ds(0, FB), lanes] = foth[g, k].T

    rowm = lax.broadcasted_iota(jnp.int32, (32, 256), 0) // 4
    lanem = lax.broadcasted_iota(jnp.int32, (32, 256), 1) // 128

    def hidden(i):
        g, cc = i // 4, rem(i, 4)
        live = rowm == 2 * cc + lanem
        for k in range(2):
            for gg in range(2):
                v = jnp.concatenate([ptt[yh if gg == 1 else 1 - yh, k]] * 2, axis=1)
                own = g == (yh if gg == 1 else 1 - yh)
                rhs[k, pl.ds(128 + 32 * gg, 32)] = jnp.where(live & own, v, 0.0).astype(BF)

        def rows(rb, _):
            r = pl.ds(pl.multiple_of(rb * HR, 16), HR)
            for t in range(2):
                ga = nn(lhs[t, 0, r], rhs[0])
                up = nn(lhs[t, 1, r], rhs[1])
                hbuf[i, t, r] = ((ga + ga * jnp.tanh(ga)) * up).astype(BF)
            return 0

        lax.fori_loop(0, FB // HR, rows, 0, unroll=HU)

    def chunk(j):
        return rem(j + 4 * (1 - yh), 8)

    sgn = 1 - 2 * c
    zn = rem(z + sgn + 8, 8)
    znd = at(x, yh, c, zn, yl)

    def part(d, i):
        return nn(dbuf[0, d], hbuf[i, 0]) + nn(dbuf[1, d], hbuf[i, 1])

    d0 = rem(z - sgn + 8, 8)

    def rsend(s, i, src):
        return rc(src, rcv.at[s, i], rs_s.at[s, i], rs_r.at[s, i], znd)


    def local_rows():
        loads[4].wait()
        for k in range(3):
            for m in range(8):
                dk[k, pl.ds(4 * m, 4)] = dtab[seeds[m], k]

        eye = lax.broadcasted_iota(jnp.int32, (128, 256), 0) == rem(lax.broadcasted_iota(jnp.int32, (128, 256), 1), 128)
        for k in range(2):
            rhs[k, 0:128] = jnp.where(eye, 1.0, 0.0).astype(BF)
            for t in range(2):
                lhs[t, k, :, pl.ds(128, 64)] = jnp.zeros((896, 64), BF)

    def base_half():
        send(bsend, brecv, bx_s, bx_r, partner)

    def base_scatter():
        bown[pl.ds(0, FB)] = partial_base(c)
        bown[pl.ds(FB, 32)] = jnp.zeros((32, 128), F32)
        recv(brecv, bx_r)
        for q in range(8):
            rows = pl.ds(112 * q, 112)
            ps[q] = (bown[rows] + brecv[rows].astype(F32)).astype(BF)
        for r in range(1, 8):
            q = rem(own_row + r, 8)
            send(ps.at[q], rsb.at[r], r1_s.at[r], r1_r.at[r], at(rem(q, 4), q // 4, c, z, yl))

    def base_sum():
        mid = pl.ds(pl.multiple_of(112 * own_row, 16), 112)
        s = bown[mid] + brecv[mid].astype(F32)
        for r in range(1, 8):
            recv(rsb.at[r], r1_r.at[r])
            s += rsb[r].astype(F32)
        s = jnp.where(c == 0, s * 0.5, s)
        bpiece(yl, c, own_row, 112)[...] = s.astype(BF)
        by_core(ag_one)

    def base_on():
        by_core(ag_two)

    def base_end():
        by_core(ag_end)
        send(lhs.at[:, c, :, pl.ds(0, 128)], lhs.at[:, c, :, pl.ds(0, 128)], bf_s, bf_r, partner)

    def base_other():
        recv(lhs.at[:, 1 - c, :, pl.ds(0, 128)], bf_r)

    def prompt_out():
        ptr = pt_v[...].astype(F32).T.astype(BF)
        psh[...] = jnp.zeros_like(psh)

        @pl.when(c == 0)
        def _():
            psh[:, 0:320] = ptr

        @pl.when(c == 1)
        def _():
            psh[:, 64:384] = ptr

        prb[c, p] = psh[toks]
        for r in range(1, 8):
            send(prb.at[c, p], prb.at[c, p], pr_s.at[r], pr_r.at[r], mate(2 * r))

    def prompt_on():
        for r in range(1, 8):
            recv(prb.at[c, rem(p - r + 8, 8)], pr_r.at[r])
        send(prb.at[c], prb.at[c], pr_s.at[0], pr_r.at[0], partner)

    def project():
        recv(prb.at[1 - c], pr_r.at[0])

        def proj_of(n, acc):
            cc, q = n // 8, rem(n, 8)
            lanes = pl.ds(pl.multiple_of(640 * q + 256 * cc, 128), 384)
            return acc + nt(prb[cc, q], dk[0:2, :, lanes].reshape(64, 384))

        acc = lax.fori_loop(0, 16, proj_of, jnp.zeros((16, 64), F32), unroll=4)
        acc = (acc / math.sqrt(D)).astype(BF).astype(F32)
        kk = lax.broadcasted_iota(jnp.int32, (16, 64), 1) // 32
        acc = jnp.where(kk == 0, acc * 0.25, acc * 0.5)
        pjs[...] = jnp.zeros_like(pjs)
        pjs[:, 0:64] = acc.astype(BF)
        pjb[yh, toks] = pjs[...]
        for r in range(1, 16):
            send(pjs, pjb.at[yh, toks], pj_s.at[r], pj_r.at[r], column(r))


    def project_in():
        for r in range(1, 16):
            hz, zz = rem(yh + r // 8, 2), rem(z - r % 8 + 8, 8)
            recv(pjb.at[hz, pl.ds(pl.multiple_of(16 * zz, 16), 16)], pj_r.at[r])
        for g in range(2):
            ptt[g] = pjb[g].astype(F32).T[0:64].reshape(2, 32, 128)

    def y_first():
        ysend(0)

    def y_second():
        ysend(1)

    def x_first():
        wait_y(0)
        own_x(0)

    def x_second():
        wait_y(1)
        own_x(1)

    def take_first():
        take[1, 0]()
        take[3, 0]()

    def take_second():
        take[1, 1]()
        take[3, 1]()

    def take_first_far():
        take[2, 0]()
        for r in range(4):
            take_d(r, 0)

    def take_second_far():
        take[2, 1]()
        for r in range(4):
            take_d(r, 1)

    def factors_far():
        for i in (0, 1):
            send(fall.at[gu, c, p], fdst(i, gu), ft_s.at[i], ft_r.at[i], fdev(i))

    def factors_near():
        send(fall.at[gu, c, p], fdst(2, gu), ft_s.at[2], ft_r.at[2], fdev(2))

    def factors_far_in():
        factors_in(False, (0, 1))
        send(fall.at[down, c, p], fdst(2, down), ft2_s.at[0], ft2_r.at[0], fdev(2))
        send(fall.at[down, c, p], fdst(0, down), ft2_s.at[1], ft2_r.at[1], fdev(0))

    def factors_near_in():
        factors_in(True, (2,))

    def hidden_ahead():
        def ahead(j, _):
            hidden(chunk(j))
            return 0

        lax.fori_loop(0, LEAD, ahead, 0)

    steps = dict(
        local_rows=local_rows,
        base_half=base_half, base_scatter=base_scatter, base_sum=base_sum, base_on=base_on, base_end=base_end,
        base_other=base_other, prompt_out=prompt_out, prompt_on=prompt_on, project=project,
        project_in=project_in, y_first=y_first, y_second=y_second, x_first=x_first, x_second=x_second,
        take_first=take_first, take_second=take_second, take_first_far=take_first_far,
        factors_far=factors_far, factors_near=factors_near, factors_far_in=factors_far_in,
        factors_near_in=factors_near_in, hidden_ahead=hidden_ahead,
    )
    for name in ORDER:
        steps[name]()

    def first(j, _):
        i = chunk(j)
        snd[i] = part(d0, i).astype(BF)
        rsend(0, i, snd.at[i]).start()

        @pl.when(j + LEAD < 8)
        def _():
            hidden(chunk(j + LEAD))

        if "take_second" not in ORDER:
            pl.when(j == TB)(take_second)

        return 0

    lax.fori_loop(0, 8, first, 0)

    for i in range(1, 8):
        q = rem(p + i, 8)
        far = q != (p + 1 - 2 * yh)
        d = rc(fall.at[:, c, p], fall.at[:, c, p], f_s.at[i], f_r.at[i], at(q // 2, rem(q, 2), c, z, yl))
        pl.when(far)(d.start)
        pending.append(functools.partial(pl.when(far), d.wait_send))
    for m in range(8):
        fitall[c, p, pl.ds(m, 1)] = jnp.full((1, 128), fit[m], F32)

    def dlanes(q, cc):
        return pl.ds(pl.multiple_of(640 * q + 256 * cc, 128), 384)

    dall[:, c, p] = dk[:, :, dlanes(p, c)]
    for r in range(1, 16):
        q, cc = rem(p + r // 2, 8), rem(c + r % 2, 2)
        send(dk.at[:, :, dlanes(q, cc)], dall.at[:, c, p], d_s.at[r], d_r.at[r], mate(r))
        send(fitall.at[c, p], fitall.at[c, p], q_s.at[r], q_r.at[r], mate(r))

    recv(frcv(2, down), ft2_r.at[0])
    tot = jnp.zeros((32, 128), F32)
    for cc in range(4):
        i = 4 * yh + cc
        q = nn(fall[2, c, p], hbuf[i, yl]) + nn(foth[yh, 2], hbuf[i, 1 - yl])
        q = jnp.where(rowm == 2 * cc + lanem, q, 0.0)
        tot += q[:, :128] + q[:, 128:]
    pdc[...] = tot.astype(BF)
    for r in range(1, 8):
        send(pdc, pdb.at[r], pd_s.at[r], pd_r.at[r], column(r))

    take_second_far()

    recv(frcv(0, down), ft2_r.at[1])
    fwd_f = rc(fall.at[:, c], fall.at[:, c], ff_s, ff_r, partner)
    pending.append(fwd_f.wait_send)

    def collect_f():
        for i in range(1, 8):
            q = rem(p - i + 8, 8)
            far = q != (p + 1 - 2 * yh)
            pl.when(far)(functools.partial(recv, fall.at[:, c, q], f_r.at[i]))
        fwd_f.start()

    def collect_d():
        for r in range(1, 16):
            q, cc = rem(p - r // 2 + 8, 8), rem(c + r % 2, 2)
            recv(dall.at[:, cc, q], d_r.at[r])
            recv(fitall.at[cc, q], q_r.at[r])
        fv = fitall[...].reshape(128, 128)
        mean = jnp.sum(fv, axis=0, keepdims=True) / 128
        spread = jnp.sum((fv - mean) ** 2, axis=0, keepdims=True) / 128
        sc = (fv - mean) / jnp.sqrt(spread + 1.0)
        for i in range(16):
            v = jnp.broadcast_to(sc[8 * i : 8 * i + 8].reshape(8, 1, 128), (8, 4, 128))
            score[i // 8, i % 8] = v.reshape(32, 128)

    def weigh(k):
        def one(g, _):
            a, b = g // 8, rem(g, 8)
            sc = score[a, b]
            w = dall[k, a, b].astype(F32) * jnp.concatenate([sc] * 3, axis=1)
            dall[k, a, b] = w.astype(BF)
            return 0
        lax.fori_loop(0, 16, one, 0)
        wt[k] = dall[k].reshape(512, 384).T

    def delta(k, half):
        r = pl.ds(pl.multiple_of(64 * c + 160 * half, 16), 160)
        v = nn(wt[k, r], fall[k].reshape(512, FB)) * (1.0 / math.sqrt(512))
        del_ref[k, pl.ds(pl.multiple_of(160 * half, 16), 160)] = v.astype(BF)

    def noise_in():
        tot = pdc[...].astype(F32)
        for r in range(1, 8):
            recv(pdb.at[r], pd_r.at[r])
            tot += pdb[r].astype(F32)
        pdt[...] = (tot / math.sqrt(FFW)).astype(BF).astype(F32) * 0.5
        a2t[...] = dk[2, :, pl.ds(pl.multiple_of(640 * z + 256 * yl, 128), 384)].T

    def noise(j):
        live = rowm == 2 * j + lanem
        pm = jnp.where(live, jnp.concatenate([pdt[...]] * 2, axis=1), 0.0).astype(BF)
        for h in range(2):
            nbuf[h, j] = nn(a2t[pl.ds(pl.multiple_of(64 * yl + 160 * h, 16), 160)], pm)

    def middle(n, _):
        s, j = n // 8 + 1, rem(n, 8)
        i = chunk(j)
        pp = part(rem(z - sgn * (1 + s) + 16, 8), i)
        recv(rcv.at[s - 1, i], rs_r.at[s - 1, i])
        rcv[s - 1, i] = (pp + rcv[s - 1, i].astype(F32)).astype(BF)
        rsend(s, i, rcv.at[s - 1, i]).start()
        rsend(s - 1, i, rcv.at[s, i]).wait_send()

        @pl.when((s == 2) & (j == 3))
        def _():
            noise_in()

        @pl.when((s == 3) & (j < 4))
        def _():
            noise(j)

        @pl.when((s == 5) & (j == 0))
        def _():
            collect_f()

        @pl.when((s == 6) & (j == 0))
        def _():
            collect_d()

        @pl.when((s == 6) & (j >= 1) & (j < 4))
        def _():
            weigh(j - 1)

        @pl.when((s == 6) & (j == 3))
        def _():
            recv(fall.at[:, 1 - c], ff_r)

        @pl.when((s == 6) & (j >= 4))
        def _():
            delta((j - 4) // 2, rem(j, 2))

        return 0

    lax.fori_loop(0, 48, middle, 0)

    def last(j):
        i = chunk(j)
        pp = part(z, i)
        recv(rcv.at[6, i], rs_r.at[6, i])
        return pp + rcv[6, i].astype(F32)

    def last_far(j, _):
        fsnd[j] = last(j).astype(BF)
        rc(fsnd.at[j], fin.at[j], fs_s.at[j], fs_r.at[j], ypart).start()

        @pl.when(j < 2)
        def _():
            delta(2, j)

        return 0

    lax.fori_loop(0, 4, last_far, 0)

    def put(j, h, w):
        for m in range(2):
            out_ref[2 * j + m, pl.ds(pl.multiple_of(160 * h, 16), 160)] = w[:, 128 * m : 128 * (m + 1)].astype(BF)

    def last_near(j, _):
        put(j, yh, last(j + 4) + nbuf[yh, j])
        return 0

    lax.fori_loop(0, 4, last_near, 0)

    def finish(j, _):
        rc(fsnd.at[j], fin.at[j], fs_s.at[j], fs_r.at[j], ypart).wait()
        put(j, 1 - yh, fin[j].astype(F32) + nbuf[1 - yh, j])
        return 0

    lax.fori_loop(0, 4, finish, 0)

    for w in pending:
        w()

    def drain(i, _):
        rsend(6, i, snd.at[i]).wait_send()
        return 0

    lax.fori_loop(0, 8, drain, 0)


def call_step(*arrays):
    arrays = [pltpu.with_memory_space_constraint(v, pltpu.HBM) for v in arrays]
    v = pl.BlockSpec(memory_space=pltpu.VMEM)
    a = pl.BlockSpec(memory_space=pltpu.HBM)
    sm = pl.BlockSpec(memory_space=pltpu.SMEM)
    dma = pltpu.SemaphoreType.DMA
    vm = pltpu.VMEM
    return pl.pallas_call(
        step_kernel,
        out_shape=[
            jax.ShapeDtypeStruct((8, 320, 128), BF),
            jax.ShapeDtypeStruct((3, 320, FB), BF),
        ],
        in_specs=[a, a, a, a, a, a, sm, sm],
        out_specs=[v, v],
        scratch_shapes=[
            vm((320, 128), BF), vm((2, 320, FB), BF), vm((2, 160, FB), BF), vm((16, 3, 4, D), BF), vm((16, 3, 4, FB), BF),
            vm((3, 32, D), BF), vm((3, 2, 8, 32, FB), BF), vm((2, 3, 32, FB), BF),
            vm((2, 8, 160, FB), BF), vm((8, 2, FB, 256), BF), vm((8, 160, 256), BF),
            vm((7, 8, 160, 256), BF), vm((4, 160, 256), BF), vm((4, 160, 256), BF),
            vm((896, 128), BF), vm((896, 128), BF), vm((896, 128), F32), vm((8, 112, 128), BF),
            vm((8, 112, 128), BF), vm((2, 2, 896, 192), BF), vm((2, 192, 256), BF),
            vm((128, 384), BF), vm((2, 8, 16, 384), BF), vm((16, 128), BF), vm((2, 128, 128), BF),
            vm((2, 2, 32, 128), F32),
            vm((32, 128), BF), vm((8, 32, 128), BF), vm((32, 128), F32), vm((3, 2, 8, 32, 384), BF),
            vm((2, 8, 8, 128), F32), vm((2, 8, 32, 128), F32), vm((3, 384, 512), BF), vm((384, 32), BF), vm((2, 4, 160, 256), F32),
            dma((6,)), dma(()), dma(()), dma((8,)), dma((8,)), dma((4,)), dma((4,)), dma((4, 4)), dma((4, 4)), dma(()), dma(()),
            dma((8,)), dma((8,)), dma((16,)), dma((16,)),
            dma((3,)), dma((3,)), dma((2,)), dma((2,)), dma((2,)), dma((2,)), dma(()), dma((2, 2)), dma((4, 2)), dma((4, 2)),
            dma((4, 2)), dma((4, 2)), dma((7, 8)), dma((7, 8)), dma((4,)), dma((4,)),
            dma((8,)), dma((8,)), dma((8,)), dma((8,)), dma(()), dma(()), dma((16,)), dma((16,)),
            dma((16,)), dma((16,)),
        ],
        compiler_params=pltpu.CompilerParams(
            collective_id=0, has_side_effects=True, vmem_limit_bytes=44 << 20
        ),
        name="es_step",
    )(*arrays)


EMIT_LIM = 4 << 20


def emit_kernel(out, deltas, o_hbm, g_hbm, u_hbm, d_hbm, sems):
    pairs = [(deltas.at[0], g_hbm), (deltas.at[1], u_hbm), (deltas.at[2], d_hbm), (out, o_hbm)]
    copies = [pltpu.make_async_copy(a, b, sems.at[i]) for i, (a, b) in enumerate(pairs)]
    for d in copies:
        d.start()
    for d in copies:
        d.wait()


def emit(out, deltas):
    v = pl.BlockSpec(memory_space=pltpu.VMEM)
    a = pl.BlockSpec(memory_space=pltpu.HBM)
    one = jax.ShapeDtypeStruct((320, FB), BF)
    return pl.pallas_call(
        emit_kernel,
        out_shape=[jax.ShapeDtypeStruct((8, 320, 128), BF), one, one, one],
        in_specs=[v, v],
        out_specs=[a, a, a, a],
        scratch_shapes=[pltpu.SemaphoreType.DMA((4,))],
        compiler_params=pltpu.CompilerParams(vmem_limit_bytes=EMIT_LIM),
        name="emit",
    )(out, deltas)


def shards(prompt_acts, gate_weight, up_weight, down_weight, d_table, f_table, seeds, fitness):
    out, deltas = call_step(
        prompt_acts.T, gate_weight, up_weight, down_weight.T.reshape(2, 160, FB), d_table, f_table,
        seeds, fitness,
    )
    out, dg, du, dd = emit(out, deltas)
    return out.transpose(0, 2, 1), dg, du, dd.T


def solution(mesh):
    split = Mesh(mesh.devices.reshape(4, 2, 2, 8, 2), AX)
    placed = (
        P(None, MEMBER), P(MEMBER, TENSOR), P(MEMBER, TENSOR), P(TENSOR, MEMBER),
        P(MEMBER, None, None, None), P(MEMBER, None, None, TENSOR), P(MEMBER), P(MEMBER),
    )
    return jax.shard_map(
        shards, mesh=split, in_specs=placed,
        out_specs=(P(MEMBER, None, TENSOR), P(MEMBER, TENSOR), P(MEMBER, TENSOR), P(TENSOR, MEMBER)),
        check_vma=False,
    )
```

time: 152 us -> 108 us (0.71)
  the two profiles are of different devices: /device:TPU:8 before, /device:TPU:1 now
where the time goes in v3:
time: 108 us; the launch traced here: 107 us
  Pallas kernels  107 us (99%)
    pallas_call x1, Pallas kernels, call_step(): pl.pallas_call(step_kernel, out_shape=[jax.ShapeDtypeStruct((8, 320, 128)...  105 us

profile of v3, /device:TPU:1, one launch (start us, length us, event | category | flops | bytes accessed | tf_op | source)
XLA Modules:
  0.0 107.2 jit_solution(11810228519511084838)
XLA Ops:
  0.6 105.1 %es_step.1 = (bf16[8,320,128]{2,1,0:T(8,128)(2,1)S(1)}, bf16[3,320,864]{2,1,0:T(8,128)(2,1)S(1)}) custom-call(bf16[320,128]{1,0:T(8,128)(2,1)} %bitcast.7, bf16[320,864]{1,0:T(8,128)(2,1)} %gw_hbm.1, bf16[320,864]{1,0:T(8,128)(2,1)} %uw_hbm.1, bf16[2,160,864]{2,1,0:T(8,128)(2,1)} %bitcast.6, bf16[16,3,4,5120]{3,2,1,0:T(4,128)(2,1)} %dtab_hbm.1, ...), custom_call_target="tpu_custom_call" | custom-call | tf_op jit(solution)/shard_map/es_step/pallas_call | solution.py:705
  105.7 1.4 %emit.1 = (bf16[8,320,128]{2,1,0:T(8,128)(2,1)}, bf16[320,864]{1,0:T(8,128)(2,1)}, bf16[320,864]{1,0:T(8,128)(2,1)}, bf16[320,864]{1,0:T(8,128)(2,1)}) custom-call(bf16[8,320,128]{2,1,0:T(8,128)(2,1)S(1)} %get-tuple-element.10.out, bf16[3,320,864]{2,1,0:T(8,128)(2,1)S(1)} %get-tuple-element.11.deltas), custom_call_target="tpu_custom_call" | custom-call | tf_op jit(solution)/shard_map/emit/pallas_call | solution.py:754

commit v4 on v3

--- a/solution.py
+++ b/solution.py
@@ -20,31 +20,45 @@
 F32 = jnp.float32
 HR = 864
 HU = 1
-LEAD = 4
+LEAD = 3
 TB = 0
+TF = 6
+CF = 32
+CD = 40
+DS = 1
 ORDER = (
     "y_first",
+    "y_first_b",
     "y_second",
     "base_half",
+    "y_second_b",
     "base_scatter",
     "prompt_out",
+    "base_mid",
+    "x_first",
+    "base_sum",
+    "x_first_b",
     "local_rows",
-    "base_sum",
     "factors_far",
+    "factors_diag",
     "prompt_on",
-    "factors_near",
-    "x_first",
+    "take_first",
     "base_on",
     "project",
-    "take_first",
+    "factors_near",
+    "take_first_b",
+    "project_in",
     "x_second",
+    "x_second_b",
     "factors_far_in",
+    "down_out",
     "base_end",
-    "project_in",
     "base_other",
+    "take_first_far",
     "hidden_ahead",
     "factors_near_in",
-    "take_first_far",
+    "take_second",
+    "first_in",
 )
 
 
@@ -69,10 +83,10 @@
 
 
 def step_kernel(
-    pt_hbm, gw_hbm, uw_hbm, dt_hbm, dtab_hbm, ftab_hbm, seeds, fit,
+    pt_hbm, gw_hbm, uw_hbm, dt_hbm, dtab_hbm, ftab_hbm, seeds_hbm, fit_hbm,
     out_ref, del_ref,
-    pt_v, w_v, dt_v, dtab, ftab, dk, fall, foth, dbuf, hbuf, snd, rcv, fin, fsnd,
-    bsend, brecv, bown, ps, rsb, lhs, rhs, psh, prb, pjs, pjb, ptt,
+    seeds, fit, pt_v, w_v, dt_v, dtab, ftab, dk, fall, foth, dbuf, hbuf, snd, rcv, fin, fsnd,
+    bsend, brecv, bown, ps, rsb, rsend2, rrecv2, lhs, rhs, psh, prb, pjs, pjb, ptt,
     pdc, pdb, pdt, dall, fitall, score, wt, a2t, nbuf,
     in_s, bx_s, bx_r, r1_s, r1_r, ag_s, ag_r, ah_s, ah_r, bf_s, bf_r, pr_s, pr_r, pj_s, pj_r,
     ft_s, ft_r, ft2_s, ft2_r, ys, yr, yloc, xo_s, xf_s, x_r, ds_s, ds_r, rs_s, rs_r, fs_s, fs_r,
@@ -101,11 +115,11 @@
 
     loads = [
         (gw_hbm, w_v.at[0]), (uw_hbm, w_v.at[1]), (pt_hbm, pt_v), (ftab_hbm, ftab), (dtab_hbm, dtab),
-        (dt_hbm, dt_v),
+        (dt_hbm, dt_v), (seeds_hbm, seeds), (fit_hbm, fit),
     ]
     loads = [pltpu.make_async_copy(a, b, in_s.at[i]) for i, (a, b) in enumerate(loads)]
-    for l in loads:
-        l.start()
+    for i in (5, 2, 0, 1, 6, 7, 3, 4):
+        loads[i].start()
 
     def plane(rel):
         ny = rem(y + rel % 4, 4)
@@ -125,27 +139,18 @@
     def greet(dev):
         pl.semaphore_signal(barrier, inc=1, device_id=dev, device_id_type=MESH)
 
-    peers = [plane(r) for r in range(1, 16)] + [mate(r) for r in range(1, 16, 2)]
+    peers = [plane(1), plane(3)] + [mate(r) for r in range(1, 16)]
     peers += [column(r) for r in range(1, 16) if r != 8]
     for o in peers:
         greet(o)
-    for h in range(2):
-        @pl.when(c != yl)
-        def _():
+    @pl.when(c != yl)
+    def _():
+        for h in range(2):
             greet(ypeers[h])
-
-    for l in loads[:3]:
-        l.wait()
 
     def partial_base(k):
         return tn(w_v[k], pt_v[...])
 
-    bsend[pl.ds(0, FB)] = partial_base(1 - c).astype(BF)
-    bsend[pl.ds(FB, 32)] = jnp.zeros((32, 128), BF)
-    loads[3].wait()
-    for k in range(3):
-        for m in range(8):
-            fall[k, c, p, pl.ds(4 * m, 4)] = ftab[seeds[m], k]
     loads[5].wait()
     n_peers = len(peers)
     @pl.when(c == yl)
@@ -168,33 +173,44 @@
 
     own_a = low(x)
 
-    def ysend(ab):
+    def half(b, part):
+        return b.at[pl.ds(80 * part, 80)]
+
+    def ycopy(h, part):
+        dst = half(dbuf.at[yl, 2 * x + yh], part)
+        return rc(half(dt_v.at[h], part), dst, ys.at[h, part], yr.at[yh, part], ypeers[h])
+
+    def ylocal(h, part):
+        return pltpu.make_async_copy(half(dt_hbm.at[h], part), half(dbuf.at[yl, 2 * x + yh], part), yloc.at[part])
+
+    def ysend(ab, part):
         mine = yh == (own_a if ab == 0 else 1 - own_a)
         for h in range(2):
             @pl.when(mine & jnp.logical_not(me_y[h]))
             def _():
-                rc(dt_v.at[h], dbuf.at[yl, 2 * x + yh], ys.at[h], yr.at[yh], ypeers[h]).start()
+                ycopy(h, part).start()
             @pl.when(mine & me_y[h])
             def _():
-                pltpu.make_async_copy(dt_hbm.at[h], dbuf.at[yl, 2 * x + yh], yloc).start()
-
-    def wait_y(ab):
+                ylocal(h, part).start()
+
+    def wait_y(ab, part):
         w = own_a if ab == 0 else 1 - own_a
         here = (w == yh) & (c == yl)
 
         @pl.when(jnp.logical_not(here))
         def _():
-            recv(dbuf.at[c, 2 * x + w], yr.at[w])
+            recv(half(dbuf.at[c, 2 * x + w], part), yr.at[w, part])
 
         @pl.when(here)
         def _():
-            pltpu.make_async_copy(dt_hbm.at[0], dbuf.at[c, 2 * x + w], yloc).wait()
+            ylocal(0, part).wait()
 
     def y_drain():
         for h in range(2):
             @pl.when(jnp.logical_not(me_y[h]))
             def _():
-                rc(dt_v.at[h], dbuf.at[yl, 2 * x + yh], ys.at[h], yr.at[yh], ypeers[h]).wait_send()
+                for part in range(2):
+                    ycopy(h, part).wait_send()
 
     pending.append(y_drain)
     xnb = [at(rem(x + 1, 4), yh, c, z, yl), at(rem(x + 3, 4), yh, c, z, yl)]
@@ -205,28 +221,31 @@
         pending.append(d.wait_send)
         return d
 
-    def own_x(ab):
+    def own_x(ab, part):
         b = dbuf.at[c, zblk(0, ab)]
-        send(b, b, xo_s.at[0, ab], x_r.at[1, ab], xnb[0])
-        send(b, b, xo_s.at[1, ab], x_r.at[3, ab], xnb[1])
-        dsend(0, ab).start()
+        if part == 1:
+            dsend(0, ab).start()
+        b = half(b, part)
+        send(b, b, xo_s.at[0, ab, part], x_r.at[1, ab, part], xnb[0])
+        send(b, b, xo_s.at[1, ab, part], x_r.at[3, ab, part], xnb[1])
 
     def taker(r, ab):
         b = dbuf.at[c, zblk(r, ab)]
         d2 = dsend(r, ab)
-        if r == 2:
-            def run():
-                recv(b, x_r.at[r, ab])
+        fwd = c == (0 if r == 1 else 1)
+        hops = []
+        for part in range(2 if r != 2 else 0):
+            h = half(b, part)
+            d = rc(h, h, xf_s.at[r, ab, part], x_r.at[2, ab, part], xnb[0 if r == 1 else 1])
+            hops.append(d)
+            pending.append(functools.partial(pl.when(fwd), d.wait_send))
+
+        def run(part):
+            recv(half(b, part), x_r.at[r, ab, part])
+            if r != 2:
+                pl.when(fwd)(hops[part].start)
+            if part == 1:
                 d2.start()
-            return run
-        fwd = c == (0 if r == 1 else 1)
-        d = rc(b, b, xf_s.at[r, ab], x_r.at[2, ab], xnb[0 if r == 1 else 1])
-        pending.append(lambda: pl.when(fwd)(d.wait_send))
-
-        def run():
-            recv(b, x_r.at[r, ab])
-            pl.when(fwd)(d.start)
-            d2.start()
 
         return run
 
@@ -351,6 +370,11 @@
 
 
     def local_rows():
+        for i in (6, 7, 3):
+            loads[i].wait()
+        for k in range(3):
+            for m in range(8):
+                fall[k, c, p, pl.ds(4 * m, 4)] = ftab[seeds[m], k]
         loads[4].wait()
         for k in range(3):
             for m in range(8):
@@ -363,6 +387,10 @@
                 lhs[t, k, :, pl.ds(128, 64)] = jnp.zeros((896, 64), BF)
 
     def base_half():
+        for i in range(3):
+            loads[i].wait()
+        bsend[pl.ds(0, FB)] = partial_base(1 - c).astype(BF)
+        bsend[pl.ds(FB, 32)] = jnp.zeros((32, 128), BF)
         send(bsend, brecv, bx_s, bx_r, partner)
 
     def base_scatter():
@@ -371,17 +399,27 @@
         recv(brecv, bx_r)
         for q in range(8):
             rows = pl.ds(112 * q, 112)
-            ps[q] = (bown[rows] + brecv[rows].astype(F32)).astype(BF)
-        for r in range(1, 8):
-            q = rem(own_row + r, 8)
-            send(ps.at[q], rsb.at[r], r1_s.at[r], r1_r.at[r], at(rem(q, 4), q // 4, c, z, yl))
+            ps[q // 4, q % 4] = (bown[rows] + brecv[rows].astype(F32)).astype(BF)
+        for r in range(1, 4):
+            xx = rem(x + r, 4)
+            send(ps.at[:, xx], rsb.at[r], r1_s.at[r], r1_r.at[r], at(xx, yh, c, z, yl))
+
+    def own_sum(h):
+        mid = pl.ds(pl.multiple_of(112 * (4 * h + x), 16), 112)
+        s = bown[mid] + brecv[mid].astype(F32)
+        for r in range(1, 4):
+            s += rsb[r, h].astype(F32)
+        return s
+
+    def base_mid():
+        for r in range(1, 4):
+            recv(rsb.at[r], r1_r.at[r])
+        rsend2[...] = own_sum(1 - yh).astype(BF)
+        send(rsend2, rrecv2, r1_s.at[0], r1_r.at[0], ypart)
 
     def base_sum():
-        mid = pl.ds(pl.multiple_of(112 * own_row, 16), 112)
-        s = bown[mid] + brecv[mid].astype(F32)
-        for r in range(1, 8):
-            recv(rsb.at[r], r1_r.at[r])
-            s += rsb[r].astype(F32)
+        recv(rrecv2, r1_r.at[0])
+        s = own_sum(yh) + rrecv2[...].astype(F32)
         s = jnp.where(c == 0, s * 0.5, s)
         bpiece(yl, c, own_row, 112)[...] = s.astype(BF)
         by_core(ag_one)
@@ -444,48 +482,80 @@
             ptt[g] = pjb[g].astype(F32).T[0:64].reshape(2, 32, 128)
 
     def y_first():
-        ysend(0)
+        ysend(0, 0)
+
+    def y_first_b():
+        ysend(0, 1)
 
     def y_second():
-        ysend(1)
+        ysend(1, 0)
+
+    def y_second_b():
+        ysend(1, 1)
 
     def x_first():
-        wait_y(0)
-        own_x(0)
+        wait_y(0, 0)
+        own_x(0, 0)
+
+    def x_first_b():
+        wait_y(0, 1)
+        own_x(0, 1)
 
     def x_second():
-        wait_y(1)
-        own_x(1)
+        wait_y(1, 0)
+        own_x(1, 0)
+
+    def x_second_b():
+        wait_y(1, 1)
+        own_x(1, 1)
+
+    def down_out():
+        send(fall.at[down, c, p], fdst(2, down), ft2_s.at[0], ft2_r.at[0], fdev(2))
+        send(fall.at[down, c, p], fdst(0, down), ft2_s.at[1], ft2_r.at[1], fdev(0))
 
     def take_first():
-        take[1, 0]()
-        take[3, 0]()
+        take[1, 0](0)
+        take[3, 0](0)
+
+    def take_first_b():
+        take[1, 0](1)
+        take[3, 0](1)
 
     def take_second():
-        take[1, 1]()
-        take[3, 1]()
+        take[1, 1](0)
+        take[3, 1](0)
+
+    def take_second_b():
+        take[1, 1](1)
+        take[3, 1](1)
 
     def take_first_far():
-        take[2, 0]()
+        for part in range(2):
+            take[2, 0](part)
+
+    def first_in():
         for r in range(4):
             take_d(r, 0)
 
     def take_second_far():
-        take[2, 1]()
+        for part in range(2):
+            take[2, 1](part)
+
+    def second_in():
         for r in range(4):
             take_d(r, 1)
 
     def factors_far():
-        for i in (0, 1):
-            send(fall.at[gu, c, p], fdst(i, gu), ft_s.at[i], ft_r.at[i], fdev(i))
+        send(fall.at[gu, c, p], fdst(0, gu), ft_s.at[0], ft_r.at[0], fdev(0))
+
+    def factors_diag():
+        send(fall.at[gu, c, p], fdst(1, gu), ft_s.at[1], ft_r.at[1], fdev(1))
 
     def factors_near():
         send(fall.at[gu, c, p], fdst(2, gu), ft_s.at[2], ft_r.at[2], fdev(2))
 
     def factors_far_in():
         factors_in(False, (0, 1))
-        send(fall.at[down, c, p], fdst(2, down), ft2_s.at[0], ft2_r.at[0], fdev(2))
-        send(fall.at[down, c, p], fdst(0, down), ft2_s.at[1], ft2_r.at[1], fdev(0))
 
     def factors_near_in():
         factors_in(True, (2,))
@@ -498,12 +568,12 @@
         lax.fori_loop(0, LEAD, ahead, 0)
 
     steps = dict(
-        local_rows=local_rows,
-        base_half=base_half, base_scatter=base_scatter, base_sum=base_sum, base_on=base_on, base_end=base_end,
+        local_rows=local_rows, down_out=down_out,
+        base_half=base_half, base_scatter=base_scatter, base_mid=base_mid, base_sum=base_sum, base_on=base_on, base_end=base_end,
         base_other=base_other, prompt_out=prompt_out, prompt_on=prompt_on, project=project,
-        project_in=project_in, y_first=y_first, y_second=y_second, x_first=x_first, x_second=x_second,
-        take_first=take_first, take_second=take_second, take_first_far=take_first_far,
-        factors_far=factors_far, factors_near=factors_near, factors_far_in=factors_far_in,
+        project_in=project_in, y_first=y_first, y_second=y_second, y_first_b=y_first_b, y_second_b=y_second_b, x_first=x_first, x_second=x_second, x_first_b=x_first_b, x_second_b=x_second_b,
+        take_first=take_first, take_first_b=take_first_b, take_second_b=take_second_b, take_second=take_second, take_first_far=take_first_far, first_in=first_in,
+        factors_far=factors_far, factors_diag=factors_diag, factors_near=factors_near, factors_far_in=factors_far_in,
         factors_near_in=factors_near_in, hidden_ahead=hidden_ahead,
     )
     for name in ORDER:
@@ -520,6 +590,9 @@
 
         if "take_second" not in ORDER:
             pl.when(j == TB)(take_second)
+        if "take_second_b" not in ORDER:
+            pl.when(j == TB)(take_second_b)
+        pl.when(j == TF)(take_second_far)
 
         return 0
 
@@ -543,18 +616,7 @@
         send(dk.at[:, :, dlanes(q, cc)], dall.at[:, c, p], d_s.at[r], d_r.at[r], mate(r))
         send(fitall.at[c, p], fitall.at[c, p], q_s.at[r], q_r.at[r], mate(r))
 
-    recv(frcv(2, down), ft2_r.at[0])
-    tot = jnp.zeros((32, 128), F32)
-    for cc in range(4):
-        i = 4 * yh + cc
-        q = nn(fall[2, c, p], hbuf[i, yl]) + nn(foth[yh, 2], hbuf[i, 1 - yl])
-        q = jnp.where(rowm == 2 * cc + lanem, q, 0.0)
-        tot += q[:, :128] + q[:, 128:]
-    pdc[...] = tot.astype(BF)
-    for r in range(1, 8):
-        send(pdc, pdb.at[r], pd_s.at[r], pd_r.at[r], column(r))
-
-    take_second_far()
+    second_in()
 
     recv(frcv(0, down), ft2_r.at[1])
     fwd_f = rc(fall.at[:, c], fall.at[:, c], ff_s, ff_r, partner)
@@ -595,6 +657,22 @@
         v = nn(wt[k, r], fall[k].reshape(512, FB)) * (1.0 / math.sqrt(512))
         del_ref[k, pl.ds(pl.multiple_of(160 * half, 16), 160)] = v.astype(BF)
 
+    pd_out = [rc(pdc, pdb.at[r], pd_s.at[r], pd_r.at[r], column(r)) for r in range(1, 8)]
+    pending.extend(d.wait_send for d in pd_out)
+
+    def down_sums():
+        recv(frcv(2, down), ft2_r.at[0])
+        tot = jnp.zeros((32, 128), F32)
+        for cc in range(4):
+            i = 4 * yh + cc
+            q = nn(fall[2, c, p], hbuf[i, yl]) + nn(foth[yh, 2], hbuf[i, 1 - yl])
+            q = jnp.where(rowm == 2 * cc + lanem, q, 0.0)
+            tot += q[:, :128] + q[:, 128:]
+        pdc[...] = tot.astype(BF)
+        for d in pd_out:
+            d.start()
+
+
     def noise_in():
         tot = pdc[...].astype(F32)
         for r in range(1, 8):
@@ -608,6 +686,8 @@
         pm = jnp.where(live, jnp.concatenate([pdt[...]] * 2, axis=1), 0.0).astype(BF)
         for h in range(2):
             nbuf[h, j] = nn(a2t[pl.ds(pl.multiple_of(64 * yl + 160 * h, 16), 160)], pm)
+
+    down_sums()
 
     def middle(n, _):
         s, j = n // 8 + 1, rem(n, 8)
@@ -618,33 +698,36 @@
         rsend(s, i, rcv.at[s - 1, i]).start()
         rsend(s - 1, i, rcv.at[s, i]).wait_send()
 
-        @pl.when((s == 2) & (j == 3))
+        @pl.when((s == 4) & (j == 3))
         def _():
             noise_in()
 
-        @pl.when((s == 3) & (j < 4))
-        def _():
-            noise(j)
-
-        @pl.when((s == 5) & (j == 0))
+        @pl.when((s == 5) & (j >= 2) & (j < 6))
+        def _():
+            noise(j - 2)
+
+        @pl.when(n == CF)
         def _():
             collect_f()
 
-        @pl.when((s == 6) & (j == 0))
+        m = n - CD
+
+        @pl.when(m == 0)
         def _():
             collect_d()
 
-        @pl.when((s == 6) & (j >= 1) & (j < 4))
-        def _():
-            weigh(j - 1)
-
-        @pl.when((s == 6) & (j == 3))
+        @pl.when((m >= 1) & (m < 4))
+        def _():
+            weigh(m - 1)
+
+        @pl.when(m == 3)
         def _():
             recv(fall.at[:, 1 - c], ff_r)
 
-        @pl.when((s == 6) & (j >= 4))
-        def _():
-            delta((j - 4) // 2, rem(j, 2))
+        @pl.when((m >= 4) & (m < 4 + 6 * DS) & (rem(m, DS) == 0))
+        def _():
+            q = (m - 4) // DS
+            delta(q // 2, rem(q, 2))
 
         return 0
 
@@ -660,9 +743,10 @@
         fsnd[j] = last(j).astype(BF)
         rc(fsnd.at[j], fin.at[j], fs_s.at[j], fs_r.at[j], ypart).start()
 
-        @pl.when(j < 2)
-        def _():
-            delta(2, j)
+        if 48 - CD - 4 < 6 * DS:
+            @pl.when(j < 2)
+            def _():
+                delta(2, j)
 
         return 0
 
@@ -699,7 +783,6 @@
     arrays = [pltpu.with_memory_space_constraint(v, pltpu.HBM) for v in arrays]
     v = pl.BlockSpec(memory_space=pltpu.VMEM)
     a = pl.BlockSpec(memory_space=pltpu.HBM)
-    sm = pl.BlockSpec(memory_space=pltpu.SMEM)
     dma = pltpu.SemaphoreType.DMA
     vm = pltpu.VMEM
     return pl.pallas_call(
@@ -708,22 +791,23 @@
             jax.ShapeDtypeStruct((8, 320, 128), BF),
             jax.ShapeDtypeStruct((3, 320, FB), BF),
         ],
-        in_specs=[a, a, a, a, a, a, sm, sm],
+        in_specs=[a] * 8,
         out_specs=[v, v],
         scratch_shapes=[
+            pltpu.SMEM((8,), jnp.int32), pltpu.SMEM((8,), F32),
             vm((320, 128), BF), vm((2, 320, FB), BF), vm((2, 160, FB), BF), vm((16, 3, 4, D), BF), vm((16, 3, 4, FB), BF),
             vm((3, 32, D), BF), vm((3, 2, 8, 32, FB), BF), vm((2, 3, 32, FB), BF),
             vm((2, 8, 160, FB), BF), vm((8, 2, FB, 256), BF), vm((8, 160, 256), BF),
             vm((7, 8, 160, 256), BF), vm((4, 160, 256), BF), vm((4, 160, 256), BF),
-            vm((896, 128), BF), vm((896, 128), BF), vm((896, 128), F32), vm((8, 112, 128), BF),
-            vm((8, 112, 128), BF), vm((2, 2, 896, 192), BF), vm((2, 192, 256), BF),
+            vm((896, 128), BF), vm((896, 128), BF), vm((896, 128), F32), vm((2, 4, 112, 128), BF),
+            vm((4, 2, 112, 128), BF), vm((112, 128), BF), vm((112, 128), BF), vm((2, 2, 896, 192), BF), vm((2, 192, 256), BF),
             vm((128, 384), BF), vm((2, 8, 16, 384), BF), vm((16, 128), BF), vm((2, 128, 128), BF),
             vm((2, 2, 32, 128), F32),
             vm((32, 128), BF), vm((8, 32, 128), BF), vm((32, 128), F32), vm((3, 2, 8, 32, 384), BF),
             vm((2, 8, 8, 128), F32), vm((2, 8, 32, 128), F32), vm((3, 384, 512), BF), vm((384, 32), BF), vm((2, 4, 160, 256), F32),
-            dma((6,)), dma(()), dma(()), dma((8,)), dma((8,)), dma((4,)), dma((4,)), dma((4, 4)), dma((4, 4)), dma(()), dma(()),
+            dma((8,)), dma(()), dma(()), dma((8,)), dma((8,)), dma((4,)), dma((4,)), dma((4, 4)), dma((4, 4)), dma(()), dma(()),
             dma((8,)), dma((8,)), dma((16,)), dma((16,)),
-            dma((3,)), dma((3,)), dma((2,)), dma((2,)), dma((2,)), dma((2,)), dma(()), dma((2, 2)), dma((4, 2)), dma((4, 2)),
+            dma((3,)), dma((3,)), dma((2,)), dma((2,)), dma((2, 2)), dma((2, 2)), dma((2,)), dma((2, 2, 2)), dma((4, 2, 2)), dma((4, 2, 2)),
             dma((4, 2)), dma((4, 2)), dma((7, 8)), dma((7, 8)), dma((4,)), dma((4,)),
             dma((8,)), dma((8,)), dma((8,)), dma((8,)), dma(()), dma(()), dma((16,)), dma((16,)),
             dma((16,)), dma((16,)),

time: 108 us -> 101 us (0.935)
  Pallas kernels: 107 us -> 99.7 us
    pallas_call x1, Pallas kernels: 105 us -> 98.3 us  [call_step(): pl.pallas_call(step_kernel, out_shape=[jax.ShapeDtypeStruct((8, 320, 128)...]
where the time goes in v4:
time: 101 us; the launch traced here: 100 us
  Pallas kernels  99.7 us (99%)
    pallas_call x1, Pallas kernels, call_step(): pl.pallas_call(step_kernel, out_shape=[jax.ShapeDtypeStruct((8, 320, 128)...  98.3 us

profile of v4, /device:TPU:1, one launch (start us, length us, event | category | flops | bytes accessed | tf_op | source)
XLA Modules:
  0.0 100.4 jit_solution(7236392769511690524)
XLA Ops:
  0.6 98.3 %es_step.1 = (bf16[8,320,128]{2,1,0:T(8,128)(2,1)S(1)}, bf16[3,320,864]{2,1,0:T(8,128)(2,1)S(1)}) custom-call(bf16[320,128]{1,0:T(8,128)(2,1)} %bitcast.7, bf16[320,864]{1,0:T(8,128)(2,1)} %gw_hbm.1, bf16[320,864]{1,0:T(8,128)(2,1)} %uw_hbm.1, bf16[2,160,864]{2,1,0:T(8,128)(2,1)} %bitcast.6, bf16[16,3,4,5120]{3,2,1,0:T(4,128)(2,1)} %dtab_hbm.1, ...), custom_call_target="tpu_custom_call" | custom-call | tf_op jit(solution)/shard_map/es_step/pallas_call | solution.py:788
  98.9 1.4 %emit.1 = (bf16[8,320,128]{2,1,0:T(8,128)(2,1)}, bf16[320,864]{1,0:T(8,128)(2,1)}, bf16[320,864]{1,0:T(8,128)(2,1)}, bf16[320,864]{1,0:T(8,128)(2,1)}) custom-call(bf16[8,320,128]{2,1,0:T(8,128)(2,1)S(1)} %get-tuple-element.10.out, bf16[3,320,864]{2,1,0:T(8,128)(2,1)S(1)} %get-tuple-element.11.deltas), custom_call_target="tpu_custom_call" | custom-call | tf_op jit(solution)/shard_map/emit/pallas_call | solution.py:838

commit v5 on v4

--- a/solution.py
+++ b/solution.py
@@ -20,11 +20,16 @@
 F32 = jnp.float32
 HR = 864
 HU = 1
-LEAD = 3
+LEAD = 1
 TB = 0
-TF = 6
-CF = 32
-CD = 40
+TB2 = 2
+TF = 7
+FX = 17
+PN = 6
+NI = 20
+CF = 35
+DX = 33
+CD = 38
 DS = 1
 ORDER = (
     "y_first",
@@ -47,17 +52,16 @@
     "project",
     "factors_near",
     "take_first_b",
-    "project_in",
     "x_second",
+    "factors_near_in",
     "x_second_b",
     "factors_far_in",
+    "base_end",
+    "take_first_far",
+    "project_in",
+    "base_other",
     "down_out",
-    "base_end",
-    "base_other",
-    "take_first_far",
     "hidden_ahead",
-    "factors_near_in",
-    "take_second",
     "first_in",
 )
 
@@ -87,7 +91,7 @@
     out_ref, del_ref,
     seeds, fit, pt_v, w_v, dt_v, dtab, ftab, dk, fall, foth, dbuf, hbuf, snd, rcv, fin, fsnd,
     bsend, brecv, bown, ps, rsb, rsend2, rrecv2, lhs, rhs, psh, prb, pjs, pjb, ptt,
-    pdc, pdb, pdt, dall, fitall, score, wt, a2t, nbuf,
+    pdc, pdb, pdt, dall, fitall, score, wt, a2t, nbuf, wbuf,
     in_s, bx_s, bx_r, r1_s, r1_r, ag_s, ag_r, ah_s, ah_r, bf_s, bf_r, pr_s, pr_r, pj_s, pj_r,
     ft_s, ft_r, ft2_s, ft2_r, ys, yr, yloc, xo_s, xf_s, x_r, ds_s, ds_r, rs_s, rs_r, fs_s, fs_r,
     pd_s, pd_r, f_s, f_r, ff_s, ff_r, d_s, d_r, q_s, q_r,
@@ -151,7 +155,10 @@
     def partial_base(k):
         return tn(w_v[k], pt_v[...])
 
-    loads[5].wait()
+    for i in (0, 1, 2, 5):
+        loads[i].wait()
+    bsend[pl.ds(0, FB)] = partial_base(1 - c).astype(BF)
+    bsend[pl.ds(FB, 32)] = jnp.zeros((32, 128), BF)
     n_peers = len(peers)
     @pl.when(c == yl)
     def _():
@@ -215,23 +222,22 @@
     pending.append(y_drain)
     xnb = [at(rem(x + 1, 4), yh, c, z, yl), at(rem(x + 3, 4), yh, c, z, yl)]
 
-    def dsend(r, ab):
-        b = dbuf.at[c, zblk(r, ab)]
-        d = rc(b, b, ds_s.at[r, ab], ds_r.at[r, ab], partner)
+    def dsend(r, ab, part):
+        b = half(dbuf.at[c, zblk(r, ab)], part)
+        d = rc(b, b, ds_s.at[r, ab, part], ds_r.at[r, ab, part], partner)
         pending.append(d.wait_send)
         return d
 
     def own_x(ab, part):
         b = dbuf.at[c, zblk(0, ab)]
-        if part == 1:
-            dsend(0, ab).start()
+        dsend(0, ab, part).start()
         b = half(b, part)
         send(b, b, xo_s.at[0, ab, part], x_r.at[1, ab, part], xnb[0])
         send(b, b, xo_s.at[1, ab, part], x_r.at[3, ab, part], xnb[1])
 
     def taker(r, ab):
         b = dbuf.at[c, zblk(r, ab)]
-        d2 = dsend(r, ab)
+        d2 = [dsend(r, ab, part) for part in range(2)]
         fwd = c == (0 if r == 1 else 1)
         hops = []
         for part in range(2 if r != 2 else 0):
@@ -244,15 +250,15 @@
             recv(half(b, part), x_r.at[r, ab, part])
             if r != 2:
                 pl.when(fwd)(hops[part].start)
-            if part == 1:
-                d2.start()
+            d2[part].start()
 
         return run
 
     take = {(r, ab): taker(r, ab) for r in (1, 3, 2) for ab in range(2)}
 
     def take_d(r, ab):
-        recv(dbuf.at[1 - c, zblk(r, ab)], ds_r.at[r, ab])
+        for part in range(2):
+            recv(half(dbuf.at[1 - c, zblk(r, ab)], part), ds_r.at[r, ab, part])
 
     toks = pl.ds(pl.multiple_of(16 * z, 16), 16)
     own_row = 4 * yh + x
@@ -334,20 +340,22 @@
     rowm = lax.broadcasted_iota(jnp.int32, (32, 256), 0) // 4
     lanem = lax.broadcasted_iota(jnp.int32, (32, 256), 1) // 128
 
+    def hidden_rows():
+        for i in range(8):
+            g, cc = i // 4, i % 4
+            for k in range(2):
+                for gg in range(2):
+                    of = yh if gg == 1 else 1 - yh
+                    v = jnp.concatenate([ptt[of, k]] * 2, axis=1)
+                    live = (rowm == 2 * cc + lanem) & (g == of)
+                    rhs[i, k, pl.ds(128 + 32 * gg, 32)] = jnp.where(live, v, 0.0).astype(BF)
+
     def hidden(i):
-        g, cc = i // 4, rem(i, 4)
-        live = rowm == 2 * cc + lanem
-        for k in range(2):
-            for gg in range(2):
-                v = jnp.concatenate([ptt[yh if gg == 1 else 1 - yh, k]] * 2, axis=1)
-                own = g == (yh if gg == 1 else 1 - yh)
-                rhs[k, pl.ds(128 + 32 * gg, 32)] = jnp.where(live & own, v, 0.0).astype(BF)
-
         def rows(rb, _):
             r = pl.ds(pl.multiple_of(rb * HR, 16), HR)
             for t in range(2):
-                ga = nn(lhs[t, 0, r], rhs[0])
-                up = nn(lhs[t, 1, r], rhs[1])
+                ga = nn(lhs[t, 0, r], rhs[i, 0])
+                up = nn(lhs[t, 1, r], rhs[i, 1])
                 hbuf[i, t, r] = ((ga + ga * jnp.tanh(ga)) * up).astype(BF)
             return 0
 
@@ -382,15 +390,12 @@
 
         eye = lax.broadcasted_iota(jnp.int32, (128, 256), 0) == rem(lax.broadcasted_iota(jnp.int32, (128, 256), 1), 128)
         for k in range(2):
-            rhs[k, 0:128] = jnp.where(eye, 1.0, 0.0).astype(BF)
+            for i in range(8):
+                rhs[i, k, 0:128] = jnp.where(eye, 1.0, 0.0).astype(BF)
             for t in range(2):
                 lhs[t, k, :, pl.ds(128, 64)] = jnp.zeros((896, 64), BF)
 
     def base_half():
-        for i in range(3):
-            loads[i].wait()
-        bsend[pl.ds(0, FB)] = partial_base(1 - c).astype(BF)
-        bsend[pl.ds(FB, 32)] = jnp.zeros((32, 128), BF)
         send(bsend, brecv, bx_s, bx_r, partner)
 
     def base_scatter():
@@ -480,6 +485,7 @@
             recv(pjb.at[hz, pl.ds(pl.multiple_of(16 * zz, 16), 16)], pj_r.at[r])
         for g in range(2):
             ptt[g] = pjb[g].astype(F32).T[0:64].reshape(2, 32, 128)
+        hidden_rows()
 
     def y_first():
         ysend(0, 0)
@@ -579,61 +585,100 @@
     for name in ORDER:
         steps[name]()
 
-    def first(j, _):
+    def step_zero(j):
         i = chunk(j)
         snd[i] = part(d0, i).astype(BF)
         rsend(0, i, snd.at[i]).start()
 
-        @pl.when(j + LEAD < 8)
-        def _():
-            hidden(chunk(j + LEAD))
-
-        if "take_second" not in ORDER:
-            pl.when(j == TB)(take_second)
-        if "take_second_b" not in ORDER:
-            pl.when(j == TB)(take_second_b)
-        pl.when(j == TF)(take_second_far)
-
+    def first(j, _):
+        i = chunk(j)
+        p0 = part(d0, i).astype(BF)
+        hidden(chunk(j + 1))
+        snd[i] = p0
+        rsend(0, i, snd.at[i]).start()
+        pl.when(j == TB)(take_second)
+        pl.when(j == TB2)(take_second_b)
         return 0
 
-    lax.fori_loop(0, 8, first, 0)
-
-    for i in range(1, 8):
-        q = rem(p + i, 8)
-        far = q != (p + 1 - 2 * yh)
-        d = rc(fall.at[:, c, p], fall.at[:, c, p], f_s.at[i], f_r.at[i], at(q // 2, rem(q, 2), c, z, yl))
-        pl.when(far)(d.start)
-        pending.append(functools.partial(pl.when(far), d.wait_send))
+    lax.fori_loop(0, 7, first, 0)
+    step_zero(7)
+    take_second_far()
+
+    recv(frcv(0, down), ft2_r.at[1])
+
+    def fpiece(i, other):
+        return fall.at[:, c, 2 * rem(x - i + 4, 4) + (1 - yh if other else yh)]
+
+    f_out, f_on = [], []
+    for i in range(1, 4):
+        f_out.append([rc(fpiece(0, h), fpiece(0, h), f_s.at[4 * h + i], f_r.at[4 * h + i], along_x[i]) for h in range(2)])
+        f_on.append(rc(fpiece(i, 0), fpiece(i, 0), f_s.at[4 + i], f_r.at[4 + i], ypart))
+
+    def factors_out(core):
+        for d in f_out:
+            for h in range(1 + core):
+                d[h].start()
+
+    def factors_drain(core):
+        for d in f_out:
+            for h in range(1 + core):
+                d[h].wait_send()
+        if core == 0:
+            for d in f_on:
+                d.wait_send()
+
+    by_core(factors_out)
+    pending.append(lambda: by_core(factors_drain))
     for m in range(8):
         fitall[c, p, pl.ds(m, 1)] = jnp.full((1, 128), fit[m], F32)
 
-    def dlanes(q, cc):
-        return pl.ds(pl.multiple_of(640 * q + 256 * cc, 128), 384)
-
-    dall[:, c, p] = dk[:, :, dlanes(p, c)]
-    for r in range(1, 16):
-        q, cc = rem(p + r // 2, 8), rem(c + r % 2, 2)
-        send(dk.at[:, :, dlanes(q, cc)], dall.at[:, c, p], d_s.at[r], d_r.at[r], mate(r))
-        send(fitall.at[c, p], fitall.at[c, p], q_s.at[r], q_r.at[r], mate(r))
+    def dlanes(q):
+        return pl.ds(pl.multiple_of(640 * q, 128), 640)
+
+    dall[:, c, p] = dk[:, :, dlanes(p)]
+    for r in range(1, 8):
+        q = rem(p + r, 8)
+        send(dk.at[:, :, dlanes(q)], dall.at[:, c, p], d_s.at[r], d_r.at[r], mate(2 * r))
+        send(fitall.at[c, p], fitall.at[c, p], q_s.at[r], q_r.at[r], mate(2 * r))
 
     second_in()
 
-    recv(frcv(0, down), ft2_r.at[1])
     fwd_f = rc(fall.at[:, c], fall.at[:, c], ff_s, ff_r, partner)
     pending.append(fwd_f.wait_send)
 
+    def factors_on():
+        @pl.when(c == 0)
+        def _():
+            for i in range(1, 4):
+                recv(fpiece(i, 0), f_r.at[i])
+            for d in f_on:
+                d.start()
+
     def collect_f():
-        for i in range(1, 8):
-            q = rem(p - i + 8, 8)
-            far = q != (p + 1 - 2 * yh)
-            pl.when(far)(functools.partial(recv, fall.at[:, c, q], f_r.at[i]))
+        @pl.when(c == 1)
+        def _():
+            for i in range(1, 4):
+                recv(fpiece(i, 0), f_r.at[i])
+
+        for i in range(1, 4):
+            recv(fpiece(i, 1), f_r.at[4 + i])
         fwd_f.start()
 
+    d_on = rc(dall.at[:, c], dall.at[:, c], d_s.at[0], d_r.at[0], partner)
+    q_on = rc(fitall.at[c], fitall.at[c], q_s.at[0], q_r.at[0], partner)
+    pending.extend([d_on.wait_send, q_on.wait_send])
+
+    def factors_d_on():
+        for r in range(1, 8):
+            q = rem(p - r + 8, 8)
+            recv(dall.at[:, c, q], d_r.at[r])
+            recv(fitall.at[c, q], q_r.at[r])
+        d_on.start()
+        q_on.start()
+
     def collect_d():
-        for r in range(1, 16):
-            q, cc = rem(p - r // 2 + 8, 8), rem(c + r % 2, 2)
-            recv(dall.at[:, cc, q], d_r.at[r])
-            recv(fitall.at[cc, q], q_r.at[r])
+        recv(dall.at[:, 1 - c], d_r.at[0])
+        recv(fitall.at[1 - c], q_r.at[0])
         fv = fitall[...].reshape(128, 128)
         mean = jnp.sum(fv, axis=0, keepdims=True) / 128
         spread = jnp.sum((fv - mean) ** 2, axis=0, keepdims=True) / 128
@@ -646,11 +691,12 @@
         def one(g, _):
             a, b = g // 8, rem(g, 8)
             sc = score[a, b]
-            w = dall[k, a, b].astype(F32) * jnp.concatenate([sc] * 3, axis=1)
-            dall[k, a, b] = w.astype(BF)
+            own = pl.ds(pl.multiple_of(256 * c, 128), 384)
+            w = dall[k, a, b, :, own].astype(F32) * jnp.concatenate([sc] * 3, axis=1)
+            wbuf[g] = w.astype(BF)
             return 0
         lax.fori_loop(0, 16, one, 0)
-        wt[k] = dall[k].reshape(512, 384).T
+        wt[k] = wbuf[...].reshape(512, 384).T
 
     def delta(k, half):
         r = pl.ds(pl.multiple_of(64 * c + 160 * half, 16), 160)
@@ -687,10 +733,15 @@
         for h in range(2):
             nbuf[h, j] = nn(a2t[pl.ds(pl.multiple_of(64 * yl + 160 * h, 16), 160)], pm)
 
-    down_sums()
+    def place(n):
+        m = n - 12
+        late = jnp.where(rem(m + 16, 8) >= 4, 1, 0)
+        s = jnp.where(n < 8, 1, jnp.where(n < 12, 2, jnp.where(n < 44, 3 + m // 8 - late, 6)))
+        j = jnp.where(n < 8, n, jnp.where(n < 12, n - 8, jnp.where(n < 44, rem(m + 16, 8), n - 40)))
+        return s, j
 
     def middle(n, _):
-        s, j = n // 8 + 1, rem(n, 8)
+        s, j = place(n)
         i = chunk(j)
         pp = part(rem(z - sgn * (1 + s) + 16, 8), i)
         recv(rcv.at[s - 1, i], rs_r.at[s - 1, i])
@@ -698,17 +749,29 @@
         rsend(s, i, rcv.at[s - 1, i]).start()
         rsend(s - 1, i, rcv.at[s, i]).wait_send()
 
-        @pl.when((s == 4) & (j == 3))
+        @pl.when(n == PN)
+        def _():
+            down_sums()
+
+        @pl.when(n == NI)
         def _():
             noise_in()
 
-        @pl.when((s == 5) & (j >= 2) & (j < 6))
-        def _():
-            noise(j - 2)
+        @pl.when((n > NI) & (n <= NI + 4))
+        def _():
+            noise(n - NI - 1)
+
+        @pl.when(n == FX)
+        def _():
+            factors_on()
 
         @pl.when(n == CF)
         def _():
             collect_f()
+
+        @pl.when(n == DX)
+        def _():
+            factors_d_on()
 
         m = n - CD
 
@@ -731,7 +794,7 @@
 
         return 0
 
-    lax.fori_loop(0, 48, middle, 0)
+    lax.fori_loop(0, 44, middle, 0)
 
     def last(j):
         i = chunk(j)
@@ -743,14 +806,10 @@
         fsnd[j] = last(j).astype(BF)
         rc(fsnd.at[j], fin.at[j], fs_s.at[j], fs_r.at[j], ypart).start()
 
-        if 48 - CD - 4 < 6 * DS:
-            @pl.when(j < 2)
-            def _():
-                delta(2, j)
-
         return 0
 
     lax.fori_loop(0, 4, last_far, 0)
+    lax.fori_loop(44, 48, middle, 0)
 
     def put(j, h, w):
         for m in range(2):
@@ -800,15 +859,15 @@
             vm((2, 8, 160, FB), BF), vm((8, 2, FB, 256), BF), vm((8, 160, 256), BF),
             vm((7, 8, 160, 256), BF), vm((4, 160, 256), BF), vm((4, 160, 256), BF),
             vm((896, 128), BF), vm((896, 128), BF), vm((896, 128), F32), vm((2, 4, 112, 128), BF),
-            vm((4, 2, 112, 128), BF), vm((112, 128), BF), vm((112, 128), BF), vm((2, 2, 896, 192), BF), vm((2, 192, 256), BF),
+            vm((4, 2, 112, 128), BF), vm((112, 128), BF), vm((112, 128), BF), vm((2, 2, 896, 192), BF), vm((8, 2, 192, 256), BF),
             vm((128, 384), BF), vm((2, 8, 16, 384), BF), vm((16, 128), BF), vm((2, 128, 128), BF),
             vm((2, 2, 32, 128), F32),
-            vm((32, 128), BF), vm((8, 32, 128), BF), vm((32, 128), F32), vm((3, 2, 8, 32, 384), BF),
-            vm((2, 8, 8, 128), F32), vm((2, 8, 32, 128), F32), vm((3, 384, 512), BF), vm((384, 32), BF), vm((2, 4, 160, 256), F32),
+            vm((32, 128), BF), vm((8, 32, 128), BF), vm((32, 128), F32), vm((3, 2, 8, 32, 640), BF),
+            vm((2, 8, 8, 128), F32), vm((2, 8, 32, 128), F32), vm((3, 384, 512), BF), vm((384, 32), BF), vm((2, 4, 160, 256), F32), vm((16, 32, 384), BF),
             dma((8,)), dma(()), dma(()), dma((8,)), dma((8,)), dma((4,)), dma((4,)), dma((4, 4)), dma((4, 4)), dma(()), dma(()),
             dma((8,)), dma((8,)), dma((16,)), dma((16,)),
             dma((3,)), dma((3,)), dma((2,)), dma((2,)), dma((2, 2)), dma((2, 2)), dma((2,)), dma((2, 2, 2)), dma((4, 2, 2)), dma((4, 2, 2)),
-            dma((4, 2)), dma((4, 2)), dma((7, 8)), dma((7, 8)), dma((4,)), dma((4,)),
+            dma((4, 2, 2)), dma((4, 2, 2)), dma((7, 8)), dma((7, 8)), dma((4,)), dma((4,)),
             dma((8,)), dma((8,)), dma((8,)), dma((8,)), dma(()), dma(()), dma((16,)), dma((16,)),
             dma((16,)), dma((16,)),
         ],

time: 101 us -> 97.4 us (0.964)
  Pallas kernels: 99.7 us -> 96.7 us
    pallas_call x1, Pallas kernels: 98.3 us -> 95.2 us  [call_step(): pl.pallas_call(step_kernel, out_shape=[jax.ShapeDtypeStruct((8, 320, 128)...]
where the time goes in v5:
time: 97.4 us; the launch traced here: 97.3 us
  Pallas kernels  96.7 us (99%)
    pallas_call x1, Pallas kernels, call_step(): pl.pallas_call(step_kernel, out_shape=[jax.ShapeDtypeStruct((8, 320, 128)...  95.2 us

profile of v5, /device:TPU:1, one launch (start us, length us, event | category | flops | bytes accessed | tf_op | source)
XLA Modules:
  0.0 97.3 jit_solution(12133879626185595664)
XLA Ops:
  0.6 95.2 %es_step.1 = (bf16[8,320,128]{2,1,0:T(8,128)(2,1)S(1)}, bf16[3,320,864]{2,1,0:T(8,128)(2,1)S(1)}) custom-call(bf16[320,128]{1,0:T(8,128)(2,1)} %bitcast.7, bf16[320,864]{1,0:T(8,128)(2,1)} %gw_hbm.1, bf16[320,864]{1,0:T(8,128)(2,1)} %uw_hbm.1, bf16[2,160,864]{2,1,0:T(8,128)(2,1)} %bitcast.6, bf16[16,3,4,5120]{3,2,1,0:T(4,128)(2,1)} %dtab_hbm.1, ...), custom_call_target="tpu_custom_call" | custom-call | tf_op jit(solution)/shard_map/es_step/pallas_call | solution.py:847
  95.9 1.4 %emit.1 = (bf16[8,320,128]{2,1,0:T(8,128)(2,1)}, bf16[320,864]{1,0:T(8,128)(2,1)}, bf16[320,864]{1,0:T(8,128)(2,1)}, bf16[320,864]{1,0:T(8,128)(2,1)}) custom-call(bf16[8,320,128]{2,1,0:T(8,128)(2,1)S(1)} %get-tuple-element.10.out, bf16[3,320,864]{2,1,0:T(8,128)(2,1)S(1)} %get-tuple-element.11.deltas), custom_call_target="tpu_custom_call" | custom-call | tf_op jit(solution)/shard_map/emit/pallas_call | solution.py:897

commit v6 on v5

--- a/solution.py
+++ b/solution.py
@@ -23,10 +23,11 @@
 LEAD = 1
 TB = 0
 TB2 = 2
-TF = 7
+TF = 5
+TF2 = 6
 FX = 17
-PN = 6
-NI = 20
+PN = 4
+NI = 30
 CF = 35
 DX = 33
 CD = 38
@@ -544,8 +545,10 @@
             take_d(r, 0)
 
     def take_second_far():
-        for part in range(2):
-            take[2, 1](part)
+        take[2, 1](0)
+
+    def take_second_far_b():
+        take[2, 1](1)
 
     def second_in():
         for r in range(4):
@@ -598,11 +601,18 @@
         rsend(0, i, snd.at[i]).start()
         pl.when(j == TB)(take_second)
         pl.when(j == TB2)(take_second_b)
+        if TF <= 6:
+            pl.when(j == TF)(take_second_far)
+        if TF2 <= 6:
+            pl.when(j == TF2)(take_second_far_b)
         return 0
 
     lax.fori_loop(0, 7, first, 0)
+    if TF > 6:
+        take_second_far()
     step_zero(7)
-    take_second_far()
+    if TF2 > 6:
+        take_second_far_b()
 
     recv(frcv(0, down), ft2_r.at[1])
 
@@ -703,8 +713,15 @@
         v = nn(wt[k, r], fall[k].reshape(512, FB)) * (1.0 / math.sqrt(512))
         del_ref[k, pl.ds(pl.multiple_of(160 * half, 16), 160)] = v.astype(BF)
 
-    pd_out = [rc(pdc, pdb.at[r], pd_s.at[r], pd_r.at[r], column(r)) for r in range(1, 8)]
+    flips = [z + 1 - 2 * rem(z, 2), z + 2 - 4 * rem(z // 2, 2), z + 4 - 8 * (z // 4)]
+    pd_out = [rc(pdc.at[k], pdb.at[k], pd_s.at[k], pd_r.at[k], at(x, yh, c, f, yl)) for k, f in enumerate(flips)]
     pending.extend(d.wait_send for d in pd_out)
+
+    def down_sum(k):
+        recv(pdb.at[k], pd_r.at[k])
+        tot = pdc[k].astype(F32) + pdb[k].astype(F32)
+        pdc[k + 1] = tot.astype(BF)
+        pd_out[k + 1].start()
 
     def down_sums():
         recv(frcv(2, down), ft2_r.at[0])
@@ -714,16 +731,13 @@
             q = nn(fall[2, c, p], hbuf[i, yl]) + nn(foth[yh, 2], hbuf[i, 1 - yl])
             q = jnp.where(rowm == 2 * cc + lanem, q, 0.0)
             tot += q[:, :128] + q[:, 128:]
-        pdc[...] = tot.astype(BF)
-        for d in pd_out:
-            d.start()
+        pdc[0] = tot.astype(BF)
+        pd_out[0].start()
 
 
     def noise_in():
-        tot = pdc[...].astype(F32)
-        for r in range(1, 8):
-            recv(pdb.at[r], pd_r.at[r])
-            tot += pdb[r].astype(F32)
+        recv(pdb.at[2], pd_r.at[2])
+        tot = pdc[2].astype(F32) + pdb[2].astype(F32)
         pdt[...] = (tot / math.sqrt(FFW)).astype(BF).astype(F32) * 0.5
         a2t[...] = dk[2, :, pl.ds(pl.multiple_of(640 * z + 256 * yl, 128), 384)].T
 
@@ -752,6 +766,9 @@
         @pl.when(n == PN)
         def _():
             down_sums()
+
+        for k in range(2):
+            pl.when(n == PN + 8 * (k + 1))(functools.partial(down_sum, k))
 
         @pl.when(n == NI)
         def _():
@@ -862,7 +879,7 @@
             vm((4, 2, 112, 128), BF), vm((112, 128), BF), vm((112, 128), BF), vm((2, 2, 896, 192), BF), vm((8, 2, 192, 256), BF),
             vm((128, 384), BF), vm((2, 8, 16, 384), BF), vm((16, 128), BF), vm((2, 128, 128), BF),
             vm((2, 2, 32, 128), F32),
-            vm((32, 128), BF), vm((8, 32, 128), BF), vm((32, 128), F32), vm((3, 2, 8, 32, 640), BF),
+            vm((3, 32, 128), BF), vm((3, 32, 128), BF), vm((32, 128), F32), vm((3, 2, 8, 32, 640), BF),
             vm((2, 8, 8, 128), F32), vm((2, 8, 32, 128), F32), vm((3, 384, 512), BF), vm((384, 32), BF), vm((2, 4, 160, 256), F32), vm((16, 32, 384), BF),
             dma((8,)), dma(()), dma(()), dma((8,)), dma((8,)), dma((4,)), dma((4,)), dma((4, 4)), dma((4, 4)), dma(()), dma(()),
             dma((8,)), dma((8,)), dma((16,)), dma((16,)),

time: 97.4 us -> 96.9 us (level)
  no operation moved by 1% of the time
where the time goes in v6:
time: 96.9 us; the launch traced here: 96.8 us
  Pallas kernels  96.2 us (99%)
    pallas_call x1, Pallas kernels, call_step(): pl.pallas_call(step_kernel, out_shape=[jax.ShapeDtypeStruct((8, 320, 128)...  94.7 us

profile of v6, /device:TPU:1, one launch (start us, length us, event | category | flops | bytes accessed | tf_op | source)
XLA Modules:
  0.0 96.8 jit_solution(12034073917443346278)
XLA Ops:
  0.6 94.7 %es_step.1 = (bf16[8,320,128]{2,1,0:T(8,128)(2,1)S(1)}, bf16[3,320,864]{2,1,0:T(8,128)(2,1)S(1)}) custom-call(bf16[320,128]{1,0:T(8,128)(2,1)} %bitcast.7, bf16[320,864]{1,0:T(8,128)(2,1)} %gw_hbm.1, bf16[320,864]{1,0:T(8,128)(2,1)} %uw_hbm.1, bf16[2,160,864]{2,1,0:T(8,128)(2,1)} %bitcast.6, bf16[16,3,4,5120]{3,2,1,0:T(4,128)(2,1)} %dtab_hbm.1, ...), custom_call_target="tpu_custom_call" | custom-call | tf_op jit(solution)/shard_map/es_step/pallas_call | solution.py:864
  95.4 1.4 %emit.1 = (bf16[8,320,128]{2,1,0:T(8,128)(2,1)}, bf16[320,864]{1,0:T(8,128)(2,1)}, bf16[320,864]{1,0:T(8,128)(2,1)}, bf16[320,864]{1,0:T(8,128)(2,1)}) custom-call(bf16[8,320,128]{2,1,0:T(8,128)(2,1)S(1)} %get-tuple-element.10.out, bf16[3,320,864]{2,1,0:T(8,128)(2,1)S(1)} %get-tuple-element.11.deltas), custom_call_target="tpu_custom_call" | custom-call | tf_op jit(solution)/shard_map/emit/pallas_call | solution.py:914

commit v7 on v6

--- a/solution.py
+++ b/solution.py
@@ -27,15 +27,15 @@
 TF2 = 6
 FX = 17
 PN = 4
-NI = 30
+NI = 32
 CF = 35
 DX = 33
 CD = 38
 DS = 1
 ORDER = (
+    "y_second",
     "y_first",
     "y_first_b",
-    "y_second",
     "base_half",
     "y_second_b",
     "base_scatter",
@@ -50,10 +50,10 @@
     "prompt_on",
     "take_first",
     "base_on",
-    "project",
     "factors_near",
     "take_first_b",
     "x_second",
+    "project",
     "factors_near_in",
     "x_second_b",
     "factors_far_in",
@@ -809,6 +809,11 @@
             q = (m - 4) // DS
             delta(q // 2, rem(q, 2))
 
+        @pl.when(n == 43)
+        def _():
+            for w in pending:
+                w()
+
         return 0
 
     lax.fori_loop(0, 44, middle, 0)
@@ -844,9 +849,6 @@
         return 0
 
     lax.fori_loop(0, 4, finish, 0)
-
-    for w in pending:
-        w()
 
     def drain(i, _):
         rsend(6, i, snd.at[i]).wait_send()

time: 96.9 us -> 96.7 us (level)
  no operation moved by 1% of the time
where the time goes in v7:
time: 96.7 us; the launch traced here: 96.6 us
  Pallas kernels  95.9 us (99%)
    pallas_call x1, Pallas kernels, call_step(): pl.pallas_call(step_kernel, out_shape=[jax.ShapeDtypeStruct((8, 320, 128)...  94.5 us

profile of v7, /device:TPU:1, one launch (start us, length us, event | category | flops | bytes accessed | tf_op | source)
XLA Modules:
  0.0 96.6 jit_solution(8359370308623550208)
XLA Ops:
  0.6 94.5 %es_step.1 = (bf16[8,320,128]{2,1,0:T(8,128)(2,1)S(1)}, bf16[3,320,864]{2,1,0:T(8,128)(2,1)S(1)}) custom-call(bf16[320,128]{1,0:T(8,128)(2,1)} %bitcast.7, bf16[320,864]{1,0:T(8,128)(2,1)} %gw_hbm.1, bf16[320,864]{1,0:T(8,128)(2,1)} %uw_hbm.1, bf16[2,160,864]{2,1,0:T(8,128)(2,1)} %bitcast.6, bf16[16,3,4,5120]{3,2,1,0:T(4,128)(2,1)} %dtab_hbm.1, ...), custom_call_target="tpu_custom_call" | custom-call | tf_op jit(solution)/shard_map/es_step/pallas_call | solution.py:866
  95.1 1.4 %emit.1 = (bf16[8,320,128]{2,1,0:T(8,128)(2,1)}, bf16[320,864]{1,0:T(8,128)(2,1)}, bf16[320,864]{1,0:T(8,128)(2,1)}, bf16[320,864]{1,0:T(8,128)(2,1)}) custom-call(bf16[8,320,128]{2,1,0:T(8,128)(2,1)S(1)} %get-tuple-element.10.out, bf16[3,320,864]{2,1,0:T(8,128)(2,1)S(1)} %get-tuple-element.11.deltas), custom_call_target="tpu_custom_call" | custom-call | tf_op jit(solution)/shard_map/emit/pallas_call | solution.py:916

commit v8 on v7

--- a/solution.py
+++ b/solution.py
@@ -21,6 +21,7 @@
 HR = 864
 HU = 1
 LEAD = 1
+BG = 1
 TB = 0
 TB2 = 2
 TF = 5
@@ -144,8 +145,8 @@
     def greet(dev):
         pl.semaphore_signal(barrier, inc=1, device_id=dev, device_id_type=MESH)
 
-    peers = [plane(1), plane(3)] + [mate(r) for r in range(1, 16)]
-    peers += [column(r) for r in range(1, 16) if r != 8]
+    peers = [column(r) for r in (4, 12, 3, 5, 11, 13, 2, 6, 10, 14, 1, 7, 9, 15)]
+    peers += [mate(r) for r in range(15, 0, -1)] + [plane(1), plane(3)]
     for o in peers:
         greet(o)
     @pl.when(c != yl)
@@ -614,7 +615,6 @@
     if TF2 > 6:
         take_second_far_b()
 
-    recv(frcv(0, down), ft2_r.at[1])
 
     def fpiece(i, other):
         return fall.at[:, c, 2 * rem(x - i + 4, 4) + (1 - yh if other else yh)]
@@ -637,19 +637,25 @@
             for d in f_on:
                 d.wait_send()
 
-    by_core(factors_out)
     pending.append(lambda: by_core(factors_drain))
-    for m in range(8):
-        fitall[c, p, pl.ds(m, 1)] = jnp.full((1, 128), fit[m], F32)
-
     def dlanes(q):
         return pl.ds(pl.multiple_of(640 * q, 128), 640)
 
-    dall[:, c, p] = dk[:, :, dlanes(p)]
+    d_out = []
     for r in range(1, 8):
         q = rem(p + r, 8)
-        send(dk.at[:, :, dlanes(q)], dall.at[:, c, p], d_s.at[r], d_r.at[r], mate(2 * r))
-        send(fitall.at[c, p], fitall.at[c, p], q_s.at[r], q_r.at[r], mate(2 * r))
+        d_out.append(rc(dk.at[:, :, dlanes(q)], dall.at[:, c, p], d_s.at[r], d_r.at[r], mate(2 * r)))
+        d_out.append(rc(fitall.at[c, p], fitall.at[c, p], q_s.at[r], q_r.at[r], mate(2 * r)))
+    pending.extend(d.wait_send for d in d_out)
+
+    def background():
+        recv(frcv(0, down), ft2_r.at[1])
+        by_core(factors_out)
+        for m in range(8):
+            fitall[c, p, pl.ds(m, 1)] = jnp.full((1, 128), fit[m], F32)
+        dall[:, c, p] = dk[:, :, dlanes(p)]
+        for d in d_out:
+            d.start()
 
     second_in()
 
@@ -762,6 +768,10 @@
         rcv[s - 1, i] = (pp + rcv[s - 1, i].astype(F32)).astype(BF)
         rsend(s, i, rcv.at[s - 1, i]).start()
         rsend(s - 1, i, rcv.at[s, i]).wait_send()
+
+        @pl.when(n == BG)
+        def _():
+            background()
 
         @pl.when(n == PN)
         def _():

time: 96.7 us -> 96.7 us (level)
  no operation moved by 1% of the time
where the time goes in v8:
time: 96.7 us; the launch traced here: 96.6 us
  Pallas kernels  96 us (99%)
    pallas_call x1, Pallas kernels, call_step(): pl.pallas_call(step_kernel, out_shape=[jax.ShapeDtypeStruct((8, 320, 128)...  94.5 us

profile of v8, /device:TPU:1, one launch (start us, length us, event | category | flops | bytes accessed | tf_op | source)
XLA Modules:
  0.0 96.6 jit_solution(12869521677554322414)
XLA Ops:
  0.6 94.5 %es_step.1 = (bf16[8,320,128]{2,1,0:T(8,128)(2,1)S(1)}, bf16[3,320,864]{2,1,0:T(8,128)(2,1)S(1)}) custom-call(bf16[320,128]{1,0:T(8,128)(2,1)} %bitcast.7, bf16[320,864]{1,0:T(8,128)(2,1)} %gw_hbm.1, bf16[320,864]{1,0:T(8,128)(2,1)} %uw_hbm.1, bf16[2,160,864]{2,1,0:T(8,128)(2,1)} %bitcast.6, bf16[16,3,4,5120]{3,2,1,0:T(4,128)(2,1)} %dtab_hbm.1, ...), custom_call_target="tpu_custom_call" | custom-call | tf_op jit(solution)/shard_map/es_step/pallas_call | solution.py:876
  95.2 1.4 %emit.1 = (bf16[8,320,128]{2,1,0:T(8,128)(2,1)}, bf16[320,864]{1,0:T(8,128)(2,1)}, bf16[320,864]{1,0:T(8,128)(2,1)}, bf16[320,864]{1,0:T(8,128)(2,1)}) custom-call(bf16[8,320,128]{2,1,0:T(8,128)(2,1)S(1)} %get-tuple-element.10.out, bf16[3,320,864]{2,1,0:T(8,128)(2,1)S(1)} %get-tuple-element.11.deltas), custom_call_target="tpu_custom_call" | custom-call | tf_op jit(solution)/shard_map/emit/pallas_call | solution.py:926

commit v9 on v7

--- a/solution.py
+++ b/solution.py
@@ -144,8 +144,8 @@
     def greet(dev):
         pl.semaphore_signal(barrier, inc=1, device_id=dev, device_id_type=MESH)
 
-    peers = [plane(1), plane(3)] + [mate(r) for r in range(1, 16)]
-    peers += [column(r) for r in range(1, 16) if r != 8]
+    peers = [column(r) for r in (4, 12, 3, 5, 11, 13, 2, 6, 10, 14, 1, 7, 9, 15)]
+    peers += [mate(r) for r in range(15, 0, -1)] + [plane(1), plane(3)]
     for o in peers:
         greet(o)
     @pl.when(c != yl)
@@ -156,10 +156,6 @@
     def partial_base(k):
         return tn(w_v[k], pt_v[...])
 
-    for i in (0, 1, 2, 5):
-        loads[i].wait()
-    bsend[pl.ds(0, FB)] = partial_base(1 - c).astype(BF)
-    bsend[pl.ds(FB, 32)] = jnp.zeros((32, 128), BF)
     n_peers = len(peers)
     @pl.when(c == yl)
     def _():
@@ -186,7 +182,7 @@
 
     def ycopy(h, part):
         dst = half(dbuf.at[yl, 2 * x + yh], part)
-        return rc(half(dt_v.at[h], part), dst, ys.at[h, part], yr.at[yh, part], ypeers[h])
+        return rc(half(dt_hbm.at[h], part), dst, ys.at[h, part], yr.at[yh, part], ypeers[h])
 
     def ylocal(h, part):
         return pltpu.make_async_copy(half(dt_hbm.at[h], part), half(dbuf.at[yl, 2 * x + yh], part), yloc.at[part])
@@ -397,6 +393,10 @@
                 lhs[t, k, :, pl.ds(128, 64)] = jnp.zeros((896, 64), BF)
 
     def base_half():
+        for i in (0, 1, 2, 5):
+            loads[i].wait()
+        bsend[pl.ds(0, FB)] = partial_base(1 - c).astype(BF)
+        bsend[pl.ds(FB, 32)] = jnp.zeros((32, 128), BF)
         send(bsend, brecv, bx_s, bx_r, partner)
 
     def base_scatter():

time: 96.7 us -> 96.9 us (level)
  no operation moved by 1% of the time
where the time goes in v9:
time: 96.9 us; the launch traced here: 96.8 us
  Pallas kernels  96.2 us (99%)
    pallas_call x1, Pallas kernels, call_step(): pl.pallas_call(step_kernel, out_shape=[jax.ShapeDtypeStruct((8, 320, 128)...  94.7 us

profile of v9, /device:TPU:1, one launch (start us, length us, event | category | flops | bytes accessed | tf_op | source)
XLA Modules:
  0.0 96.8 jit_solution(10421405193727941584)
XLA Ops:
  0.6 94.7 %es_step.1 = (bf16[8,320,128]{2,1,0:T(8,128)(2,1)S(1)}, bf16[3,320,864]{2,1,0:T(8,128)(2,1)S(1)}) custom-call(bf16[320,128]{1,0:T(8,128)(2,1)} %bitcast.7, bf16[320,864]{1,0:T(8,128)(2,1)} %gw_hbm.1, bf16[320,864]{1,0:T(8,128)(2,1)} %uw_hbm.1, bf16[2,160,864]{2,1,0:T(8,128)(2,1)} %bitcast.6, bf16[16,3,4,5120]{3,2,1,0:T(4,128)(2,1)} %dtab_hbm.1, ...), custom_call_target="tpu_custom_call" | custom-call | tf_op jit(solution)/shard_map/es_step/pallas_call | solution.py:866
  95.4 1.4 %emit.1 = (bf16[8,320,128]{2,1,0:T(8,128)(2,1)}, bf16[320,864]{1,0:T(8,128)(2,1)}, bf16[320,864]{1,0:T(8,128)(2,1)}, bf16[320,864]{1,0:T(8,128)(2,1)}) custom-call(bf16[8,320,128]{2,1,0:T(8,128)(2,1)S(1)} %get-tuple-element.10.out, bf16[3,320,864]{2,1,0:T(8,128)(2,1)S(1)} %get-tuple-element.11.deltas), custom_call_target="tpu_custom_call" | custom-call | tf_op jit(solution)/shard_map/emit/pallas_call | solution.py:916
